TPU v7x, 32 devices: a whole 2x2x4 slice. The times are simulated.
32 devices in a mesh: tok: 16 (over z, y, x), head: 2 (over core).
Axes of the slice: x: 2, y: 2, z: 4, core: 2. Of those that a mesh axis runs over, the one named last changes fastest.
Arguments:
- query_rows: bfloat16 [6144, 2048], P('tok', 'head'), may hold values from -6 to 6
- key_rows: bfloat16 [6144, 1024], P('tok', 'head'), may hold values from -6 to 6
- value_rows: bfloat16 [6144, 1024], P('tok', 'head'), may hold values from -6 to 6
- out_grad: bfloat16 [6144, 2048], P('tok', 'head'), may hold values from -96 to 96
- log_norm: float32 [6144, 16], P('tok', 'head'), may hold values from 6.5 to 8
- delta_rows: float32 [6144, 16], P('tok', 'head'), may hold values from -48 to 48
- window_len: int32 [16], P('head'), may hold values from 896 to 1024, as said below
- activations: bfloat16 [6144, 5376], P('tok'), may hold values from -6 to 6
- value_weight: bfloat16 [5376, 1024], P('tok', 'head')
- row_state: float32 [2, 5376], P('head', 'tok'), as said below
- col_state: float32 [16, 1024], P('tok', 'head'), as said below
Outputs:
- query_grad: bfloat16 [6144, 2048], P('tok', 'head')
- key_grad: bfloat16 [6144, 1024], P('tok', 'head')
- value_grad: bfloat16 [6144, 1024], P('tok', 'head')
- new_weight: bfloat16 [5376, 1024], P('tok', 'head')
- update_dir: float32 [5376, 1024], P('tok', 'head')
Inputs may be any that keep to these rules, and one draw needn't show every extreme that they name: `window_len`: every head's window is one of the integers from 896 to 1024, and some head has exactly 1024. `row_state`: positive. `col_state`: positive.
All inputs are finite; a program needn't handle non-finite values.
Results may differ from a plain program's by a relative error of at most 0.005.
Values may be sent and summed in bfloat16 or wider, within the bound.
A program may use at most 128 MiB of HBM per device.

v0:
```python
import functools
import math

import jax
import jax.numpy as jnp
from jax import lax
from jax.experimental import pallas as pl
from jax.experimental.pallas import tpu as pltpu
from jax.sharding import PartitionSpec as P

HD = 128
WINDOW = 1024
WINDOW_MIN = 896
SUB = 128
QUERY_SCALE = 1.0 / 12.0
LOG2E = math.log2(math.e)
DECAY_RATE = 0.9
LEARN_RATE = 0.05
F32 = jnp.float32
BF16 = jnp.bfloat16
MESH = pl.DeviceIdType.MESH


def xor(index, j):
    k = 0
    while (1 << k) <= j:
        if (j >> k) & 1:
            index = index + (1 << k) * (1 - 2 * lax.rem(index // (1 << k), 2))
        k += 1
    return index


class Plan:
    def __init__(self, n, n_head, tok_len, kv_local, group, width, rows):
        self.n, self.n_head, self.tok_len = n, n_head, tok_len
        self.kv_local, self.group = kv_local, group
        self.width, self.rows = width, rows
        self.gather = 4 if n % 4 == 0 else 1
        self.upper = n // self.gather
        self.split = self.gather if kv_local % self.gather == 0 else 1
        self.kv = kv_local // self.split
        self.tokens = self.split * tok_len
        self.blocks = n // self.split
        self.reach = min(-(-WINDOW // self.tokens), self.blocks - 1)
        self.subs = tok_len // SUB
        self.streams = self.split
        self.part = width // self.streams
        self.bits = int(math.log2(self.upper))
        self.share = 2 if n_head % 2 == 0 and self.upper % 2 == 0 else 1

    def halo_count(self, o):
        return min(self.tokens, WINDOW - (o - 1) * self.tokens)

    def halo_first(self, o):
        return max(0, WINDOW - o * self.tokens)


def fused_kernel(
    pn,
    lim_ref, q_ref, g_ref, k_ref, v_ref, st_ref, at_ref, w_ref, rs_ref, cs_ref,
    dq_ref, dk_ref, dv_ref, sc_ref, fac_ref,
    qb, gb, kb, vb, stb, dva, dka, dqb, dkb, hsv, hsk, hrv, hrk, act, vga, acc, sbuf, rbuf,
    xs, xr,
    own_sem, in_s, in_r, halo_s, halo_r, back_s, back_r, act_own, act_s, act_r, fwd_s, fwd_r,
    vg_s, vg_r, dq_s, dq_r, dk_s, dk_r, out_sem, rs_s, rs_r, x_s, x_r,
):
    n, n_head, gather, upper = pn.n, pn.n_head, pn.gather, pn.upper
    split, kv, length, tokens = pn.split, pn.kv, pn.tok_len, pn.tokens
    group, subs = pn.group, pn.subs
    me, hd = lax.axis_index("tok"), lax.axis_index("head")
    c, u = lax.rem(me, gather), me // gather
    place, block = lax.rem(me, split), me // split
    kw, qw = kv * HD, kv * group * HD

    def at_plane(j):
        return {"tok": me - c + xor(c, j)}

    near = [(j, h) for j in range(gather) for h in range(n_head) if j or h]
    far = list(range(1, upper))
    near_ids = [{"tok": me - c + xor(c, j), "head": xor(hd, h)} for j, h in near]
    far_ids = [{"tok": xor(u, i) * gather + c} for i in far]
    barrier = pltpu.get_barrier_semaphore()
    for partner in near_ids + far_ids:
        pl.semaphore_signal(barrier, inc=1, device_id=partner, device_id_type=MESH)
    lone = []
    if split == 1:
        for o in range(1, pn.reach + 1):
            lone.append(o)
            @pl.when(block + o < pn.blocks)
            def _(o=o):
                pl.semaphore_signal(barrier, inc=1, device_id={"tok": me + o}, device_id_type=MESH)

            @pl.when(block >= o)
            def _(o=o):
                pl.semaphore_signal(barrier, inc=1, device_id={"tok": me - o}, device_id_type=MESH)

    def cols(index, size):
        return pl.ds(pl.multiple_of(index * size, 128), size)

    own = [
        pltpu.make_async_copy(k_ref.at[:, cols(place, kw)], kb.at[pl.ds(WINDOW + place * length, length)], own_sem.at[0]),
        pltpu.make_async_copy(v_ref.at[:, cols(place, kw)], vb.at[pl.ds(WINDOW + place * length, length)], own_sem.at[1]),
        pltpu.make_async_copy(q_ref.at[:, cols(place, qw)], qb.at[pl.ds(place * length, length)], own_sem.at[2]),
        pltpu.make_async_copy(g_ref.at[:, cols(place, qw)], gb.at[pl.ds(place * length, length)], own_sem.at[3]),
        pltpu.make_async_copy(st_ref.at[pl.ds(place * kv, kv)], stb.at[place], own_sem.at[4]),
    ]
    for copy in own:
        copy.start()
    half = upper // pn.share
    low = lax.rem(hd, pn.share) * half

    act_mine = [
        pltpu.make_async_copy(
            at_ref.at[i * gather + c], act.at[i, :, cols(c, length)], act_own.at[i]
        )
        for i in range(upper)
    ]
    for copy in act_mine:
        copy.start()
    dva[...] = jnp.zeros_like(dva)
    dka[...] = jnp.zeros_like(dka)

    pl.semaphore_wait(barrier, len(near_ids) + len(far_ids))
    for o in lone:
        @pl.when(block + o < pn.blocks)
        def _():
            pl.semaphore_wait(barrier, 1)

        @pl.when(block >= o)
        def _():
            pl.semaphore_wait(barrier, 1)

    def exchange(a, j):
        other = xor(place, j)
        src, dst = [
            (k_ref.at[:, cols(other, kw)], kb.at[pl.ds(WINDOW + place * length, length)]),
            (v_ref.at[:, cols(other, kw)], vb.at[pl.ds(WINDOW + place * length, length)]),
            (q_ref.at[:, cols(other, qw)], qb.at[pl.ds(place * length, length)]),
            (g_ref.at[:, cols(other, qw)], gb.at[pl.ds(place * length, length)]),
            (st_ref.at[pl.ds(other * kv, kv)], stb.at[place]),
        ][a]
        return pltpu.make_async_remote_copy(
            src_ref=src, dst_ref=dst, send_sem=in_s.at[a, j], recv_sem=in_r.at[a, j],
            device_id=at_plane(j), device_id_type=MESH,
        )

    for a in (0, 1, 4, 2, 3):
        for j in range(1, split):
            exchange(a, j).start()

    def halo(a, o):
        count, first = pn.halo_count(o), pn.halo_first(o)
        buf = (kb, vb)[a]
        return pltpu.make_async_remote_copy(
            src_ref=buf.at[pl.ds(WINDOW + tokens - count, count)],
            dst_ref=buf.at[pl.ds(first, count)],
            send_sem=halo_s.at[a, o - 1], recv_sem=halo_r.at[a, o - 1],
            device_id={"tok": me + o * split}, device_id_type=MESH,
        )

    for a in (0, 1):
        own[a].wait()
        for j in range(1, split):
            exchange(a, j).wait_recv()
        for o in range(1, pn.reach + 1):
            @pl.when(block + o < pn.blocks)
            def _(a=a, o=o):
                halo(a, o).start()

            @pl.when(block < o)
            def _(a=a, o=o):
                buf = (kb, vb)[a]
                here = pl.ds(pn.halo_first(o), pn.halo_count(o))
                buf[here] = jnp.zeros((pn.halo_count(o), kw), BF16)
    if pn.reach * tokens < WINDOW:
        rest = WINDOW - pn.reach * tokens
        for buf in (kb, vb):
            buf[pl.ds(0, rest)] = jnp.zeros((rest, kw), BF16)

    def act_send(j, i):
        other = xor(c, j)
        return pltpu.make_async_remote_copy(
            src_ref=at_ref.at[(low + i) * gather + other],
            dst_ref=act.at[low + i, :, cols(c, length)],
            send_sem=act_s.at[j, i], recv_sem=act_r.at[j, i],
            device_id=at_plane(j), device_id_type=MESH,
        )

    def act_forward(j):
        piece = act.at[pl.ds(low, half), :, cols(xor(c, j), length)]
        return pltpu.make_async_remote_copy(
            src_ref=piece, dst_ref=piece, send_sem=fwd_s.at[j], recv_sem=fwd_r.at[j],
            device_id={"head": xor(hd, 1)}, device_id_type=MESH,
        )

    for a in (0, 1):
        for o in range(1, pn.reach + 1):
            @pl.when(block >= o)
            def _(a=a, o=o):
                halo(a, o).wait_recv()

    seen = WINDOW + SUB
    chunk = seen // 3
    lanes = group * SUB

    def unit(b, kh, sub):
        start = pl.multiple_of(b * length + sub * SUB, SUB)
        rows_q = pl.ds(start, SUB)
        head = kh * group * HD
        query = jnp.concatenate(
            [qb[rows_q, head + m * HD : head + (m + 1) * HD] for m in range(group)], axis=0
        )
        grad = jnp.concatenate(
            [gb[rows_q, head + m * HD : head + (m + 1) * HD] for m in range(group)], axis=0
        )
        norm = stb[b, kh, pl.ds(sub, 1), :]
        delta = stb[b, kh, pl.ds(subs + sub, 1), :]
        total = jnp.zeros((lanes, HD), F32)
        for piece in range(3):
            here = pl.ds(pl.multiple_of(start + piece * chunk, SUB), chunk)
            keys = kb[here, kh * HD : (kh + 1) * HD]
            values = vb[here, kh * HD : (kh + 1) * HD]
            scores = lax.dot_general(
                keys, query, (((1,), (1,)), ((), ())), preferred_element_type=F32
            )
            prob = jnp.exp2(scores * (QUERY_SCALE * LOG2E) - norm)
            if piece == 0:
                edge = WINDOW - WINDOW_MIN + SUB
                row = lax.broadcasted_iota(jnp.int32, (edge, lanes), 0)
                lane = lax.broadcasted_iota(jnp.int32, (edge, lanes), 1)
                limit = jnp.full((edge, lanes), 0, jnp.int32)
                for m in range(group):
                    limit = jnp.where(
                        lane // SUB == m, lim_ref[(place * kv + kh) * group + m], limit
                    )
                visible = WINDOW + lax.rem(lane, SUB) - row < limit
                prob = jnp.concatenate(
                    [jnp.where(visible, prob[:edge], 0.0), prob[edge:]], axis=0
                )
            if piece == 2:
                row = lax.broadcasted_iota(jnp.int32, (SUB, lanes), 0)
                lane = lax.broadcasted_iota(jnp.int32, (SUB, lanes), 1)
                visible = row <= lax.rem(lane, SUB)
                prob = jnp.concatenate(
                    [prob[: chunk - SUB], jnp.where(visible, prob[chunk - SUB :], 0.0)], axis=0
                )
            dva[here, kh * HD : (kh + 1) * HD] += jnp.dot(
                prob.astype(BF16), grad, preferred_element_type=F32
            )
            dprob = lax.dot_general(
                values, grad, (((1,), (1,)), ((), ())), preferred_element_type=F32
            )
            dscore = (QUERY_SCALE * prob * (dprob - delta)).astype(BF16)
            dka[here, kh * HD : (kh + 1) * HD] += jnp.dot(
                dscore, query, preferred_element_type=F32
            )
            total = total + lax.dot_general(
                dscore, keys, (((0,), (0,)), ((), ())), preferred_element_type=F32
            )
        low_q = total.astype(BF16)
        for m in range(group):
            dqb[rows_q, head + m * HD : head + (m + 1) * HD] = low_q[m * SUB : (m + 1) * SUB]

    def dq_send(j):
        other = xor(place, j)
        src = dqb.at[pl.ds(other * length, length)]
        return pltpu.make_async_remote_copy(
            src_ref=src, dst_ref=dq_ref.at[:, cols(place, qw)],
            send_sem=dq_s.at[j], recv_sem=dq_r.at[j],
            device_id=at_plane(j), device_id_type=MESH,
        )

    def local_out(src, dst, i):
        return pltpu.make_async_copy(src, dst, out_sem.at[i])

    for j in range(split):
        b = xor(place, j)
        for a in (2, 3, 4):
            if j:
                exchange(a, j).wait_recv()
            else:
                own[a].wait()
        for kh in range(kv):
            @pl.loop(0, subs)
            def _(sub, b=b, kh=kh):
                unit(b, kh, sub)

        if j == 0:
            for jj in range(1, gather):
                for i in range(half):
                    act_send(jj, i).start()

    def back(a, o):
        count, first = pn.halo_count(o), pn.halo_first(o)
        return pltpu.make_async_remote_copy(
            src_ref=(hsv, hsk)[a].at[pl.ds(first, count)],
            dst_ref=(hrv, hrk)[a].at[o - 1, pl.ds(0, count)],
            send_sem=back_s.at[a, o - 1], recv_sem=back_r.at[a, o - 1],
            device_id={"tok": me - o * split}, device_id_type=MESH,
        )

    for a in (0, 1):
        (hsv, hsk)[a][...] = (dva, dka)[a][pl.ds(0, WINDOW)].astype(BF16)
        for o in range(1, pn.reach + 1):
            @pl.when(block >= o)
            def _(a=a, o=o):
                back(a, o).start()

    def add_back(a):
        for o in range(1, pn.reach + 1):
            @pl.when(block + o < pn.blocks)
            def _(o=o):
                count = pn.halo_count(o)
                back(a, o).wait_recv()
                here = pl.ds(WINDOW + tokens - count, count)
                total = (dva, dka)[a]
                total[here] = total[here] + (hrv, hrk)[a][o - 1, pl.ds(0, count)].astype(F32)

    def vg_send(j):
        return pltpu.make_async_remote_copy(
            src_ref=vga.at[c], dst_ref=vga.at[c], send_sem=vg_s.at[j], recv_sem=vg_r.at[j],
            device_id=at_plane(j), device_id_type=MESH,
        )

    add_back(0)
    vga[c] = dva[pl.ds(WINDOW, tokens)].astype(BF16)
    for j in range(1, gather):
        vg_send(j).start()

    local = 0
    outs = []
    outs.append(local_out(dqb.at[pl.ds(place * length, length)], dq_ref.at[:, cols(place, qw)], 0))
    outs[-1].start()
    for j in range(1, split):
        dq_send(j).start()

    add_back(1)
    dkb[...] = dka[pl.ds(WINDOW, tokens)].astype(BF16)

    def dk_send(j):
        other = xor(place, j)
        return pltpu.make_async_remote_copy(
            src_ref=dkb.at[pl.ds(other * length, length)], dst_ref=dk_ref.at[:, cols(place, kw)],
            send_sem=dk_s.at[j], recv_sem=dk_r.at[j],
            device_id=at_plane(j), device_id_type=MESH,
        )

    outs.append(local_out(dkb.at[pl.ds(place * length, length)], dk_ref.at[:, cols(place, kw)], 1))
    outs[-1].start()
    for j in range(1, split):
        dk_send(j).start()

    for copy in act_mine:
        copy.wait()
    for j in range(1, gather):
        for i in range(half):
            act_send(j, i).wait_recv()
        if pn.share == 2:
            act_forward(j).start()
    if pn.share == 2:
        for j in range(1, gather):
            piece_in = act.at[pl.ds(half - low, half), :, cols(xor(c, j), length)]
            pltpu.make_async_remote_copy(
                src_ref=piece_in, dst_ref=piece_in, send_sem=fwd_s.at[j], recv_sem=fwd_r.at[j],
                device_id={"head": xor(hd, 1)}, device_id_type=MESH,
            ).wait_recv()

    bits, part, rows = pn.bits, pn.part, pn.rows
    counts = [upper >> (p + 1) for p in range(bits)]
    starts = [sum(counts[:p]) for p in range(bits)]
    partners = [{"tok": xor(u, 1 << p) * gather + c} for p in range(bits)]

    def bit_of(index, k):
        return lax.rem(index // (1 << k), 2)

    def block_at(phase, j, other):
        index = 0
        for k in range(phase):
            index = index + (1 << k) * bit_of(u, k)
        mine = bit_of(u, phase)
        index = index + (1 << phase) * ((1 - mine) if other else mine)
        return index + (1 << (phase + 1)) * j

    def copy_of(s, p):
        here = pl.ds(starts[p], counts[p])
        return pltpu.make_async_remote_copy(
            src_ref=sbuf.at[s, here], dst_ref=rbuf.at[s, here],
            send_sem=rs_s.at[s, p], recv_sem=rs_r.at[s, p],
            device_id=partners[p], device_id_type=MESH,
        )

    def product(s, index):
        if split == gather:
            return jnp.dot(act[index], vga[xor(c, s)], preferred_element_type=F32)
        whole = vga[...].reshape(gather * length, part)
        return jnp.dot(act[index], whole, preferred_element_type=F32)

    def wait_vg(j):
        vg_in = vga.at[xor(c, j)]
        pltpu.make_async_remote_copy(
            src_ref=vg_in, dst_ref=vg_in, send_sem=vg_s.at[j], recv_sem=vg_r.at[j],
            device_id=at_plane(j), device_id_type=MESH,
        ).wait_recv()

    if split == 1:
        for j in range(1, gather):
            wait_vg(j)
    for s in range(pn.streams):
        if s:
            wait_vg(s)

        @pl.loop(0, counts[0])
        def _(j, s=s):
            sbuf[s, j] = product(s, block_at(0, j, True)).astype(BF16)

        copy_of(s, 0).start()

        @pl.loop(0, counts[0])
        def _(j, s=s):
            index = block_at(0, j, False)
            acc[s, index] = product(s, index)

    if split == gather:
        for j in range(gather):
            src = xor(c, j)
            outs.append(local_out(
                vga.at[src, pl.ds(c * length, length)], dv_ref.at[:, cols(src, kw)], 2 + j))
            outs[-1].start()
    else:
        outs.append(local_out(vga.at[c], dv_ref, 2))
        outs[-1].start()

    weight_f = w_ref[...].astype(F32)
    weight_sum = jnp.sum(weight_f * weight_f)

    for p in range(bits):
        for s in range(pn.streams):
            copy_of(s, p).wait_recv()

            @pl.loop(0, counts[p])
            def _(j, s=s, p=p):
                index = block_at(p, j, False)
                acc[s, index] = acc[s, index] + rbuf[s, starts[p] + j].astype(F32)

            if p + 1 < bits:
                @pl.loop(0, counts[p + 1])
                def _(j, s=s, p=p):
                    index = block_at(p + 1, j, True)
                    sbuf[s, starts[p + 1] + j] = acc[s, index].astype(BF16)

                copy_of(s, p + 1).start()

    row_sum = jnp.zeros((rows, 1), F32)
    for s in range(pn.streams):
        wg = acc[s, u]
        row_sum = row_sum + jnp.sum(wg * wg, axis=1, keepdims=True)
    row_mix = DECAY_RATE * rs_ref[...] + (1.0 - DECAY_RATE) * (row_sum / pn.width)
    row_mean = jnp.sum(row_mix) / rows
    scaled_sum = jnp.float32(0.0)
    for s in range(pn.streams):
        wg = acc[s, u]
        here = cols(xor(c, s), part) if split == gather else slice(0, part)
        col_new = jnp.sum(wg * wg, axis=0, keepdims=True) / rows
        col_mix = DECAY_RATE * cs_ref[:, here] + (1.0 - DECAY_RATE) * col_new
        scaled = wg / jnp.sqrt(row_mix * col_mix / row_mean)
        sc_ref[:, here] = scaled
        scaled_sum = scaled_sum + jnp.sum(scaled * scaled)

    row = lax.broadcasted_iota(jnp.int32, (8, 128), 0)
    xs[0] = jnp.where(row < 4, scaled_sum, weight_sum)

    def share(level, i, partner):
        slot = i + (len(near) if level else 0)
        return pltpu.make_async_remote_copy(
            src_ref=xs.at[level], dst_ref=xr.at[slot], send_sem=x_s.at[slot],
            recv_sem=x_r.at[slot], device_id=partner, device_id_type=MESH,
        )

    for level, ids in enumerate((near_ids, far_ids)):
        for i, partner in enumerate(ids):
            share(level, i, partner).start()
        total = xs[level]
        for i, partner in enumerate(ids):
            share(level, i, partner).wait_recv()
            total = total + xr[i + (len(near) if level else 0)]
        xs[level + 1] = total
    sums = xs[2]
    size = float(rows * n * pn.width * n_head)
    rms_scaled = jnp.sqrt(sums[0:1] / size)
    rms_weight = jnp.sqrt(sums[4:5] / size)
    fac_ref[...] = jnp.broadcast_to(rms_weight / jnp.maximum(1.0, rms_scaled), fac_ref.shape)

    for a in range(5):
        for j in range(1, split):
            exchange(a, j).wait_send()
    for a in (0, 1):
        for o in range(1, pn.reach + 1):
            @pl.when(block + o < pn.blocks)
            def _(a=a, o=o):
                halo(a, o).wait_send()

            @pl.when(block >= o)
            def _(a=a, o=o):
                back(a, o).wait_send()
    for j in range(1, gather):
        for i in range(half):
            act_send(j, i).wait_send()
        if pn.share == 2:
            act_forward(j).wait_send()
        vg_send(j).wait_send()
    for j in range(1, split):
        dq_send(j).wait()
        dk_send(j).wait()
    for copy in outs:
        copy.wait()
    for p in range(bits):
        for s in range(pn.streams):
            copy_of(s, p).wait_send()
    for level, ids in enumerate((near_ids, far_ids)):
        for i, partner in enumerate(ids):
            share(level, i, partner).wait_send()


def fused(pn, limits, query, grad, keys, values, stats, act_t, weight, row_state, col_state):
    kw, qw = pn.kv * HD, pn.kv * pn.group * HD
    whole = WINDOW + pn.tokens
    smem = pl.BlockSpec(memory_space=pltpu.SMEM)
    vmem = pl.BlockSpec(memory_space=pltpu.VMEM)
    hbm = pl.BlockSpec(memory_space=pl.ANY)
    dma = pltpu.SemaphoreType.DMA
    half = pn.upper // pn.share
    peers = pn.gather * pn.n_head - 1 + pn.upper - 1
    reach, gather, split = pn.reach, pn.gather, pn.split
    piece = (pn.tokens, kw) if split == gather else (pn.tok_len, kw)
    return pl.pallas_call(
        functools.partial(fused_kernel, pn),
        out_shape=[
            jax.ShapeDtypeStruct(query.shape, BF16),
            jax.ShapeDtypeStruct(keys.shape, BF16),
            jax.ShapeDtypeStruct(keys.shape, BF16),
            jax.ShapeDtypeStruct((pn.rows, pn.width), F32),
            jax.ShapeDtypeStruct((8, 128), F32),
        ],
        in_specs=[smem, vmem, vmem, vmem, vmem, vmem, hbm, vmem, vmem, vmem],
        out_specs=[hbm, hbm, hbm, vmem, vmem],
        scratch_shapes=[
            pltpu.VMEM((pn.tokens, qw), BF16),
            pltpu.VMEM((pn.tokens, qw), BF16),
            pltpu.VMEM((whole, kw), BF16),
            pltpu.VMEM((whole, kw), BF16),
            pltpu.VMEM((split, pn.kv, 2 * pn.subs, pn.group * SUB), F32),
            pltpu.VMEM((whole, kw), F32),
            pltpu.VMEM((whole, kw), F32),
            pltpu.VMEM((pn.tokens, qw), BF16),
            pltpu.VMEM((pn.tokens, kw), BF16),
            pltpu.VMEM((WINDOW, kw), BF16),
            pltpu.VMEM((WINDOW, kw), BF16),
            pltpu.VMEM((reach, min(pn.tokens, WINDOW), kw), BF16),
            pltpu.VMEM((reach, min(pn.tokens, WINDOW), kw), BF16),
            pltpu.VMEM((pn.upper, pn.rows, gather * pn.tok_len), BF16),
            pltpu.VMEM((gather,) + piece, BF16),
            pltpu.VMEM((pn.streams, pn.upper, pn.rows, pn.part), F32),
            pltpu.VMEM((pn.streams, pn.upper - 1, pn.rows, pn.part), BF16),
            pltpu.VMEM((pn.streams, pn.upper - 1, pn.rows, pn.part), BF16),
            pltpu.VMEM((3, 8, 128), F32),
            pltpu.VMEM((peers, 8, 128), F32),
            dma((5,)), dma((5, split)), dma((5, split)), dma((2, reach)), dma((2, reach)),
            dma((2, reach)), dma((2, reach)), dma((pn.upper,)),
            dma((gather, half)), dma((gather, half)), dma((gather,)), dma((gather,)),
            dma((gather,)), dma((gather,)), dma((split,)), dma((split,)),
            dma((split,)), dma((split,)), dma((2 + gather,)),
            dma((pn.streams, pn.bits)), dma((pn.streams, pn.bits)), dma((peers,)), dma((peers,)),
        ],
        compiler_params=pltpu.CompilerParams(
            collective_id=0, has_side_effects=True, vmem_limit_bytes=56 * 1024 * 1024
        ),
        name="fused",
    )(limits, query, grad, keys, values, stats, act_t, weight, row_state, col_state)


def shards(
    query_rows, key_rows, value_rows, out_grad, log_norm, delta_rows, window_len,
    activations, value_weight, row_state, col_state, *, n, n_head,
):
    tok_len = query_rows.shape[0]
    kv_local = key_rows.shape[1] // HD
    group = query_rows.shape[1] // key_rows.shape[1]
    rows, width = value_weight.shape
    pn = Plan(n, n_head, tok_len, kv_local, group, width, rows)

    def arranged(x):
        x = x.reshape(pn.subs, SUB, kv_local, group)
        return jnp.transpose(x, (2, 0, 3, 1)).reshape(kv_local, pn.subs, group * SUB)

    stats = jnp.concatenate([arranged(log_norm * LOG2E), arranged(delta_rows)], axis=1)
    act_t = activations.T.reshape(n, rows, tok_len)
    query_grad, key_grad, value_grad, scaled, factor = fused(
        pn, window_len, query_rows, out_grad, key_rows, value_rows, stats, act_t,
        value_weight, row_state.reshape(-1, 1), col_state,
    )
    update_dir = scaled * factor[0, 0]
    new_weight = (value_weight.astype(F32) - LEARN_RATE * update_dir).astype(BF16)
    return (query_grad, key_grad, value_grad, new_weight, update_dir)


def solution(mesh):
    both = P("tok", "head")
    return jax.shard_map(
        functools.partial(shards, n=mesh.shape["tok"], n_head=mesh.shape["head"]),
        mesh=mesh,
        in_specs=(
            both, both, both, both, both, both, P("head"), P("tok", None),
            both, P("head", "tok"), both,
        ),
        out_specs=(both,) * 5,
        check_vma=False,
    )
```

profile of v0, /device:TPU:0, one launch (start us, length us, event | category | flops | bytes accessed | tf_op | source)
XLA Modules:
  0.0 121.5 jit_solution(8714014508731485949)
XLA Ops:
  0.6 0.7 broadcast_multiply_fusion.1
  1.4 0.7 reshape.30
  2.1 0.6 pad_maximum_fusion.st_ref
  2.7 1.5 %copy.24.rs_ref = f32[336,1]{1,0:T(8,128)} copy(f32[336,1]{0,1:T(1,128)} %bitcast.22) | data formatting | bytes 2688 | tf_op jit(solution)/shard_map/reshape | solution.py:599
  4.2 6.4 %copy.23 = bf16[5376,384]{1,0:T(8,128)(2,1)} copy(bf16[5376,384]{0,1:T(8,128)(2,1)} %bitcast.17) | data formatting | bytes 8257536 | tf_op jit(solution)/shard_map/transpose | solution.py:596
  10.6 0.0 copy-start
  10.6 102.2 %fused.1 = (bf16[384,1024]{1,0:T(8,128)(2,1)}, bf16[384,512]{1,0:T(8,128)(2,1)}, bf16[384,512]{1,0:T(8,128)(2,1)}, f32[336,512]{1,0:T(8,128)}, f32[8,128]{1,0:T(8,128)}) custom-call(s32[8]{0:T(128)} %lim_ref.1, bf16[384,1024]{1,0:T(8,128)(2,1)} %q_ref.1, bf16[384,1024]{1,0:T(8,128)(2,1)} %g_ref.1, bf16[384,512]{1,0:T(8,128)(2,1)} %k_ref.1, ...), custom_call_target="tpu_custom_call" | custom-call | tf_op jit(solution)/shard_map/fused/pallas_call | solution.py:535
  112.8 0.0 copy-start.1
  112.8 1.2 %slice.3 = f32[1,1]{1,0:T(1,128)} slice(f32[8,128]{1,0:T(8,128)} %get-tuple-element.14), slice={[0:1], [0:1]} | slice | bytes 8 | tf_op jit(solution)/shard_map/slice | solution.py:601
  114.0 0.0 copy-done
  114.0 2.8 %subtract_convert_fusion = (bf16[336,512]{1,0:T(8,128)(2,1)}, f32[336,512]{1,0:T(8,128)}) fusion(bf16[336,512]{1,0:T(8,128)(2,1)S(1)} %copy-done, f32[336,512]{1,0:T(8,128)} %get-tuple-element.13, f32[]{:T(128)} %bitcast.7), kind=kLoop, calls=%fused_computation | loop fusion | flops 860160 | bytes 2064388 | tf_op jit(solution)/shard_map/convert_element_type | solution.py:602
  116.9 2.1 %copy.32 = bf16[384,1024]{1,0:T(8,128)(2,1)} copy(bf16[384,1024]{1,0:T(8,128)(2,1)} %get-tuple-element.22) | data formatting | bytes 1572864
  118.9 1.8 %copy.33 = bf16[384,512]{1,0:T(8,128)(2,1)} copy(bf16[384,512]{1,0:T(8,128)(2,1)} %get-tuple-element.23) | data formatting | bytes 786432
  120.7 0.0 copy-done.1
  120.7 0.7 copy.34
  (5 shorter events, 0.0 us)
Async XLA Ops:
  10.6 103.4 %copy-start = (bf16[336,512]{1,0:T(8,128)(2,1)S(1)}, bf16[336,512]{1,0:T(8,128)(2,1)}, u32[]{:S(2)}) copy-start(bf16[336,512]{1,0:T(8,128)(2,1)} %w_ref.1) | copy-start | bytes 1032196
  112.8 7.9 %copy-start.1 = (bf16[384,512]{1,0:T(8,128)(2,1)S(1)}, bf16[384,512]{1,0:T(8,128)(2,1)}, u32[]{:S(2)}) copy-start(bf16[384,512]{1,0:T(8,128)(2,1)} %get-tuple-element.24) | copy-start | bytes 1179652
where the time goes:
time: 122 us; the launch traced here: 121 us
  Pallas kernels  102 us (84%)
  local copies, waits for them, and re-layouts  14.5 us (12%)
  other arithmetic  4.17 us (3%)
    pallas_call x1, Pallas kernels, fused(): pl.pallas_call(functools.partial(fused_kernel, pn), out_shape=[jax.ShapeD...  102 us
    transpose x1, local copies, waits for them, and re-layouts, shards(): act_t = activations.T.reshape(n, rows, tok_len)  6.4 us
    unnamed x7, local copies, waits for them, and re-layouts  4.58 us
    convert_element_type x1, other arithmetic, shards(): (value_weight.astype(F32) - LEARN_RATE * update_dir).astype(BF16)  2.83 us

commit v1 on v0

--- a/solution.py
+++ b/solution.py
@@ -47,6 +47,9 @@
         self.part = width // self.streams
         self.bits = int(math.log2(self.upper))
         self.share = 2 if n_head % 2 == 0 and self.upper % 2 == 0 else 1
+        self.half = self.upper // self.share
+        self.wide = self.half * self.gather * rows
+        self.inside = rows % 16 == 0 and self.wide % SUB == 0
 
     def halo_count(self, o):
         return min(self.tokens, WINDOW - (o - 1) * self.tokens)
@@ -55,11 +58,36 @@
         return max(0, WINDOW - o * self.tokens)
 
 
+class Link:
+    def __init__(self, ledger, key, src, dst, sems, at, device, send_if=None, recv_if=None):
+        self.ledger, self.key = ledger, key
+        self.send_if, self.recv_if = send_if, recv_if
+        self.copy = pltpu.make_async_remote_copy(
+            src_ref=src, dst_ref=dst, send_sem=sems[0].at[at], recv_sem=sems[1].at[at],
+            device_id=device, device_id_type=MESH,
+        )
+
+    def guarded(self, condition, action):
+        if condition is None:
+            action()
+        else:
+            pl.when(condition)(action)
+
+    def start(self):
+        self.guarded(self.send_if, self.copy.start)
+        self.ledger[self.key + ("send",)] = lambda: self.guarded(self.send_if, self.copy.wait_send)
+        self.ledger[self.key + ("recv",)] = lambda: self.guarded(self.recv_if, self.copy.wait_recv)
+
+    def wait_recv(self):
+        self.ledger.pop(self.key + ("recv",))
+        self.guarded(self.recv_if, self.copy.wait_recv)
+
+
 def fused_kernel(
     pn,
-    lim_ref, q_ref, g_ref, k_ref, v_ref, st_ref, at_ref, w_ref, rs_ref, cs_ref,
+    lim_ref, q_ref, g_ref, k_ref, v_ref, ln_ref, de_ref, at_ref, w_ref, rs_ref, cs_ref,
     dq_ref, dk_ref, dv_ref, sc_ref, fac_ref,
-    qb, gb, kb, vb, stb, dva, dka, dqb, dkb, hsv, hsk, hrv, hrk, act, vga, acc, sbuf, rbuf,
+    st, wv, abuf, turned, qb, gb, kb, vb, stb, dva, dka, dqb, dkb, hsv, hsk, hrv, hrk, act, vga, acc, sbuf, rbuf,
     xs, xr,
     own_sem, in_s, in_r, halo_s, halo_r, back_s, back_r, act_own, act_s, act_r, fwd_s, fwd_r,
     vg_s, vg_r, dq_s, dq_r, dk_s, dk_r, out_sem, rs_s, rs_r, x_s, x_r,
@@ -71,6 +99,8 @@
     c, u = lax.rem(me, gather), me // gather
     place, block = lax.rem(me, split), me // split
     kw, qw = kv * HD, kv * group * HD
+    rows = pn.rows
+    ledger = {}
 
     def at_plane(j):
         return {"tok": me - c + xor(c, j)}
@@ -102,23 +132,19 @@
         pltpu.make_async_copy(v_ref.at[:, cols(place, kw)], vb.at[pl.ds(WINDOW + place * length, length)], own_sem.at[1]),
         pltpu.make_async_copy(q_ref.at[:, cols(place, qw)], qb.at[pl.ds(place * length, length)], own_sem.at[2]),
         pltpu.make_async_copy(g_ref.at[:, cols(place, qw)], gb.at[pl.ds(place * length, length)], own_sem.at[3]),
-        pltpu.make_async_copy(st_ref.at[pl.ds(place * kv, kv)], stb.at[place], own_sem.at[4]),
+        pltpu.make_async_copy(st.at[pl.ds(place * kv, kv)], stb.at[place], own_sem.at[4]),
     ]
-    for copy in own:
+    half = pn.half
+    low = lax.rem(hd, pn.share) * half
+    if pn.inside:
+        load = pltpu.make_async_copy(
+            at_ref.at[:, cols(lax.rem(hd, pn.share), pn.wide)], abuf, own_sem.at[5]
+        )
+        load.start()
+    for copy in own[:4]:
         copy.start()
-    half = upper // pn.share
-    low = lax.rem(hd, pn.share) * half
-
-    act_mine = [
-        pltpu.make_async_copy(
-            at_ref.at[i * gather + c], act.at[i, :, cols(c, length)], act_own.at[i]
-        )
-        for i in range(upper)
-    ]
-    for copy in act_mine:
-        copy.start()
-    dva[...] = jnp.zeros_like(dva)
-    dka[...] = jnp.zeros_like(dka)
+    weight_in = pltpu.make_async_copy(w_ref, wv, own_sem.at[6])
+    weight_in.start()
 
     pl.semaphore_wait(barrier, len(near_ids) + len(far_ids))
     for o in lone:
@@ -137,25 +163,42 @@
             (v_ref.at[:, cols(other, kw)], vb.at[pl.ds(WINDOW + place * length, length)]),
             (q_ref.at[:, cols(other, qw)], qb.at[pl.ds(place * length, length)]),
             (g_ref.at[:, cols(other, qw)], gb.at[pl.ds(place * length, length)]),
-            (st_ref.at[pl.ds(other * kv, kv)], stb.at[place]),
+            (st.at[pl.ds(other * kv, kv)], stb.at[place]),
         ][a]
-        return pltpu.make_async_remote_copy(
-            src_ref=src, dst_ref=dst, send_sem=in_s.at[a, j], recv_sem=in_r.at[a, j],
-            device_id=at_plane(j), device_id_type=MESH,
-        )
-
-    for a in (0, 1, 4, 2, 3):
+        return Link(ledger, ("in", a, j), src, dst, (in_s, in_r), (a, j), at_plane(j))
+
+    for a in (0, 1, 2, 3):
         for j in range(1, split):
             exchange(a, j).start()
+    for i, ref in enumerate((ln_ref, de_ref)):
+        stat = ref[...]
+        if i == 0:
+            stat = stat * LOG2E
+        for k in range(pn.kv_local):
+            st[k, i * group : (i + 1) * group] = stat[k * group : (k + 1) * group]
+    own[4].start()
+    for j in range(1, split):
+        exchange(4, j).start()
+    dva[...] = jnp.zeros_like(dva)
+    dka[...] = jnp.zeros_like(dka)
+
+    def turn(first, last):
+        @pl.loop(first, last)
+        def _(i):
+            here = pl.ds(pl.multiple_of(i * SUB, SUB), SUB)
+            turned[here, :] = abuf[:, here].T
+
+    steps = pn.wide // SUB
+    if pn.inside:
+        load.wait()
 
     def halo(a, o):
         count, first = pn.halo_count(o), pn.halo_first(o)
         buf = (kb, vb)[a]
-        return pltpu.make_async_remote_copy(
-            src_ref=buf.at[pl.ds(WINDOW + tokens - count, count)],
-            dst_ref=buf.at[pl.ds(first, count)],
-            send_sem=halo_s.at[a, o - 1], recv_sem=halo_r.at[a, o - 1],
-            device_id={"tok": me + o * split}, device_id_type=MESH,
+        return Link(
+            ledger, ("halo", a, o), buf.at[pl.ds(WINDOW + tokens - count, count)],
+            buf.at[pl.ds(first, count)], (halo_s, halo_r), (a, o - 1), {"tok": me + o * split},
+            block + o < pn.blocks, block >= o,
         )
 
     for a in (0, 1):
@@ -163,9 +206,7 @@
         for j in range(1, split):
             exchange(a, j).wait_recv()
         for o in range(1, pn.reach + 1):
-            @pl.when(block + o < pn.blocks)
-            def _(a=a, o=o):
-                halo(a, o).start()
+            halo(a, o).start()
 
             @pl.when(block < o)
             def _(a=a, o=o):
@@ -177,27 +218,37 @@
         for buf in (kb, vb):
             buf[pl.ds(0, rest)] = jnp.zeros((rest, kw), BF16)
 
+    if pn.inside:
+        turn(0, steps)
+
+    def act_piece(i, owner):
+        if pn.inside:
+            return turned.at[pl.ds(pl.multiple_of((i * gather + owner) * rows, 16), rows)]
+        return at_ref.at[(low + i) * gather + owner]
+
+    act_mine = [
+        pltpu.make_async_copy(act_piece(i, c), act.at[low + i, :, cols(c, length)], act_own.at[i])
+        for i in range(half)
+    ]
+    for copy in act_mine:
+        copy.start()
+
     def act_send(j, i):
-        other = xor(c, j)
-        return pltpu.make_async_remote_copy(
-            src_ref=at_ref.at[(low + i) * gather + other],
-            dst_ref=act.at[low + i, :, cols(c, length)],
-            send_sem=act_s.at[j, i], recv_sem=act_r.at[j, i],
-            device_id=at_plane(j), device_id_type=MESH,
+        return Link(
+            ledger, ("act", j, i), act_piece(i, xor(c, j)), act.at[low + i, :, cols(c, length)],
+            (act_s, act_r), (j, i), at_plane(j),
         )
 
     def act_forward(j):
         piece = act.at[pl.ds(low, half), :, cols(xor(c, j), length)]
-        return pltpu.make_async_remote_copy(
-            src_ref=piece, dst_ref=piece, send_sem=fwd_s.at[j], recv_sem=fwd_r.at[j],
-            device_id={"head": xor(hd, 1)}, device_id_type=MESH,
-        )
-
+        return Link(ledger, ("forward", j), piece, piece, (fwd_s, fwd_r), (j,), {"head": xor(hd, 1)})
+
+    for i in range(half):
+        for j in range(1, gather):
+            act_send(j, i).start()
     for a in (0, 1):
         for o in range(1, pn.reach + 1):
-            @pl.when(block >= o)
-            def _(a=a, o=o):
-                halo(a, o).wait_recv()
+            halo(a, o).wait_recv()
 
     seen = WINDOW + SUB
     chunk = seen // 3
@@ -213,8 +264,11 @@
         grad = jnp.concatenate(
             [gb[rows_q, head + m * HD : head + (m + 1) * HD] for m in range(group)], axis=0
         )
-        norm = stb[b, kh, pl.ds(sub, 1), :]
-        delta = stb[b, kh, pl.ds(subs + sub, 1), :]
+        lane_q = pl.ds(pl.multiple_of(sub * SUB, SUB), SUB)
+        norm, delta = [
+            jnp.concatenate([stb[b, kh, i * group + m : i * group + m + 1, lane_q] for m in range(group)], axis=1)
+            for i in range(2)
+        ]
         total = jnp.zeros((lanes, HD), F32)
         for piece in range(3):
             here = pl.ds(pl.multiple_of(start + piece * chunk, SUB), chunk)
@@ -264,11 +318,8 @@
     def dq_send(j):
         other = xor(place, j)
         src = dqb.at[pl.ds(other * length, length)]
-        return pltpu.make_async_remote_copy(
-            src_ref=src, dst_ref=dq_ref.at[:, cols(place, qw)],
-            send_sem=dq_s.at[j], recv_sem=dq_r.at[j],
-            device_id=at_plane(j), device_id_type=MESH,
-        )
+        return Link(
+            ledger, ("dq", j), src, dq_ref.at[:, cols(place, qw)], (dq_s, dq_r), (j,), at_plane(j))
 
     def local_out(src, dst, i):
         return pltpu.make_async_copy(src, dst, out_sem.at[i])
@@ -286,86 +337,71 @@
                 unit(b, kh, sub)
 
         if j == 0:
-            for jj in range(1, gather):
-                for i in range(half):
-                    act_send(jj, i).start()
+            for copy in act_mine:
+                copy.wait()
+            if pn.share == 2:
+                act_forward(0).start()
 
     def back(a, o):
         count, first = pn.halo_count(o), pn.halo_first(o)
-        return pltpu.make_async_remote_copy(
-            src_ref=(hsv, hsk)[a].at[pl.ds(first, count)],
-            dst_ref=(hrv, hrk)[a].at[o - 1, pl.ds(0, count)],
-            send_sem=back_s.at[a, o - 1], recv_sem=back_r.at[a, o - 1],
-            device_id={"tok": me - o * split}, device_id_type=MESH,
+        return Link(
+            ledger, ("back", a, o), (hsv, hsk)[a].at[pl.ds(first, count)],
+            (hrv, hrk)[a].at[o - 1, pl.ds(0, count)], (back_s, back_r), (a, o - 1),
+            {"tok": me - o * split}, block >= o, block + o < pn.blocks,
         )
 
     for a in (0, 1):
         (hsv, hsk)[a][...] = (dva, dka)[a][pl.ds(0, WINDOW)].astype(BF16)
         for o in range(1, pn.reach + 1):
-            @pl.when(block >= o)
-            def _(a=a, o=o):
-                back(a, o).start()
+            back(a, o).start()
 
     def add_back(a):
         for o in range(1, pn.reach + 1):
+            back(a, o).wait_recv()
+
             @pl.when(block + o < pn.blocks)
             def _(o=o):
                 count = pn.halo_count(o)
-                back(a, o).wait_recv()
                 here = pl.ds(WINDOW + tokens - count, count)
                 total = (dva, dka)[a]
                 total[here] = total[here] + (hrv, hrk)[a][o - 1, pl.ds(0, count)].astype(F32)
 
-    def vg_send(j):
-        return pltpu.make_async_remote_copy(
-            src_ref=vga.at[c], dst_ref=vga.at[c], send_sem=vg_s.at[j], recv_sem=vg_r.at[j],
-            device_id=at_plane(j), device_id_type=MESH,
-        )
+    cut = vga.shape[1] // 2
+
+    def vg_copy(j, owner, part_of):
+        piece = vga.at[owner, pl.ds(part_of * cut, cut)]
+        return Link(
+            ledger, ("vg", j, part_of), piece, piece, (vg_s, vg_r), (j, part_of),
+            at_plane(j if j < 3 else (2, 1)[part_of]),
+        )
+
+    def vg_send(j, h):
+        return vg_copy(j, c if j < 3 else xor(c, (1, 2)[h]), h)
+
+    def vg_wait(j, h):
+        vg_copy(j, xor(c, j), h).wait_recv()
 
     add_back(0)
     vga[c] = dva[pl.ds(WINDOW, tokens)].astype(BF16)
-    for j in range(1, gather):
-        vg_send(j).start()
-
-    local = 0
-    outs = []
-    outs.append(local_out(dqb.at[pl.ds(place * length, length)], dq_ref.at[:, cols(place, qw)], 0))
-    outs[-1].start()
-    for j in range(1, split):
-        dq_send(j).start()
-
-    add_back(1)
-    dkb[...] = dka[pl.ds(WINDOW, tokens)].astype(BF16)
-
-    def dk_send(j):
-        other = xor(place, j)
-        return pltpu.make_async_remote_copy(
-            src_ref=dkb.at[pl.ds(other * length, length)], dst_ref=dk_ref.at[:, cols(place, kw)],
-            send_sem=dk_s.at[j], recv_sem=dk_r.at[j],
-            device_id=at_plane(j), device_id_type=MESH,
-        )
-
-    outs.append(local_out(dkb.at[pl.ds(place * length, length)], dk_ref.at[:, cols(place, kw)], 1))
-    outs[-1].start()
-    for j in range(1, split):
-        dk_send(j).start()
-
-    for copy in act_mine:
-        copy.wait()
+    if gather > 1:
+        for h in (0, 1):
+            vg_send(1, h).start()
+            vg_send(2, 1 - h).start()
     for j in range(1, gather):
         for i in range(half):
             act_send(j, i).wait_recv()
         if pn.share == 2:
             act_forward(j).start()
+
     if pn.share == 2:
-        for j in range(1, gather):
+        for j in range(gather):
             piece_in = act.at[pl.ds(half - low, half), :, cols(xor(c, j), length)]
-            pltpu.make_async_remote_copy(
-                src_ref=piece_in, dst_ref=piece_in, send_sem=fwd_s.at[j], recv_sem=fwd_r.at[j],
-                device_id={"head": xor(hd, 1)}, device_id_type=MESH,
+            Link(
+                ledger, ("forward", j), piece_in, piece_in, (fwd_s, fwd_r), (j,),
+                {"head": xor(hd, 1)},
             ).wait_recv()
 
-    bits, part, rows = pn.bits, pn.part, pn.rows
+    bits, part = pn.bits, pn.part
     counts = [upper >> (p + 1) for p in range(bits)]
     starts = [sum(counts[:p]) for p in range(bits)]
     partners = [{"tok": xor(u, 1 << p) * gather + c} for p in range(bits)]
@@ -383,11 +419,8 @@
 
     def copy_of(s, p):
         here = pl.ds(starts[p], counts[p])
-        return pltpu.make_async_remote_copy(
-            src_ref=sbuf.at[s, here], dst_ref=rbuf.at[s, here],
-            send_sem=rs_s.at[s, p], recv_sem=rs_r.at[s, p],
-            device_id=partners[p], device_id_type=MESH,
-        )
+        return Link(
+            ledger, ("sum", s, p), sbuf.at[s, here], rbuf.at[s, here], (rs_s, rs_r), (s, p), partners[p])
 
     def product(s, index):
         if split == gather:
@@ -395,19 +428,26 @@
         whole = vga[...].reshape(gather * length, part)
         return jnp.dot(act[index], whole, preferred_element_type=F32)
 
-    def wait_vg(j):
-        vg_in = vga.at[xor(c, j)]
-        pltpu.make_async_remote_copy(
-            src_ref=vg_in, dst_ref=vg_in, send_sem=vg_s.at[j], recv_sem=vg_r.at[j],
-            device_id=at_plane(j), device_id_type=MESH,
-        ).wait_recv()
-
-    if split == 1:
-        for j in range(1, gather):
-            wait_vg(j)
+    def pass_on():
+        vg_wait(1, 0)
+        vg_send(3, 0).start()
+        vg_wait(2, 1)
+        vg_send(3, 1).start()
+
+    if split == 1 and gather > 1:
+        pass_on()
+        vg_wait(1, 1)
+        vg_wait(2, 0)
+        vg_wait(3, 0)
+        vg_wait(3, 1)
     for s in range(pn.streams):
-        if s:
-            wait_vg(s)
+        if s == 1:
+            pass_on()
+        if s == 3:
+            vg_wait(3, 0)
+            vg_wait(3, 1)
+        elif s:
+            vg_wait(s, s % 2)
 
         @pl.loop(0, counts[0])
         def _(j, s=s):
@@ -420,6 +460,26 @@
             index = block_at(0, j, False)
             acc[s, index] = product(s, index)
 
+    outs = []
+    outs.append(local_out(dqb.at[pl.ds(place * length, length)], dq_ref.at[:, cols(place, qw)], 0))
+    outs[-1].start()
+    for j in range(1, split):
+        dq_send(j).start()
+
+    add_back(1)
+    dkb[...] = dka[pl.ds(WINDOW, tokens)].astype(BF16)
+
+    def dk_send(j):
+        other = xor(place, j)
+        return Link(
+            ledger, ("dk", j), dkb.at[pl.ds(other * length, length)], dk_ref.at[:, cols(place, kw)],
+            (dk_s, dk_r), (j,), at_plane(j),
+        )
+
+    outs.append(local_out(dkb.at[pl.ds(place * length, length)], dk_ref.at[:, cols(place, kw)], 1))
+    outs[-1].start()
+    for j in range(1, split):
+        dk_send(j).start()
     if split == gather:
         for j in range(gather):
             src = xor(c, j)
@@ -430,7 +490,8 @@
         outs.append(local_out(vga.at[c], dv_ref, 2))
         outs[-1].start()
 
-    weight_f = w_ref[...].astype(F32)
+    weight_in.wait()
+    weight_f = wv[...].astype(F32)
     weight_sum = jnp.sum(weight_f * weight_f)
 
     for p in range(bits):
@@ -454,7 +515,10 @@
     for s in range(pn.streams):
         wg = acc[s, u]
         row_sum = row_sum + jnp.sum(wg * wg, axis=1, keepdims=True)
-    row_mix = DECAY_RATE * rs_ref[...] + (1.0 - DECAY_RATE) * (row_sum / pn.width)
+    diag = lax.broadcasted_iota(jnp.int32, (rows, rows), 0) == lax.broadcasted_iota(
+        jnp.int32, (rows, rows), 1)
+    row_old = jnp.sum(jnp.where(diag, rs_ref[...], 0.0), axis=1, keepdims=True)
+    row_mix = DECAY_RATE * row_old + (1.0 - DECAY_RATE) * (row_sum / pn.width)
     row_mean = jnp.sum(row_mix) / rows
     scaled_sum = jnp.float32(0.0)
     for s in range(pn.streams):
@@ -471,10 +535,7 @@
 
     def share(level, i, partner):
         slot = i + (len(near) if level else 0)
-        return pltpu.make_async_remote_copy(
-            src_ref=xs.at[level], dst_ref=xr.at[slot], send_sem=x_s.at[slot],
-            recv_sem=x_r.at[slot], device_id=partner, device_id_type=MESH,
-        )
+        return Link(ledger, ("share", slot), xs.at[level], xr.at[slot], (x_s, x_r), (slot,), partner)
 
     for level, ids in enumerate((near_ids, far_ids)):
         for i, partner in enumerate(ids):
@@ -490,45 +551,20 @@
     rms_weight = jnp.sqrt(sums[4:5] / size)
     fac_ref[...] = jnp.broadcast_to(rms_weight / jnp.maximum(1.0, rms_scaled), fac_ref.shape)
 
-    for a in range(5):
-        for j in range(1, split):
-            exchange(a, j).wait_send()
-    for a in (0, 1):
-        for o in range(1, pn.reach + 1):
-            @pl.when(block + o < pn.blocks)
-            def _(a=a, o=o):
-                halo(a, o).wait_send()
-
-            @pl.when(block >= o)
-            def _(a=a, o=o):
-                back(a, o).wait_send()
-    for j in range(1, gather):
-        for i in range(half):
-            act_send(j, i).wait_send()
-        if pn.share == 2:
-            act_forward(j).wait_send()
-        vg_send(j).wait_send()
-    for j in range(1, split):
-        dq_send(j).wait()
-        dk_send(j).wait()
     for copy in outs:
         copy.wait()
-    for p in range(bits):
-        for s in range(pn.streams):
-            copy_of(s, p).wait_send()
-    for level, ids in enumerate((near_ids, far_ids)):
-        for i, partner in enumerate(ids):
-            share(level, i, partner).wait_send()
-
-
-def fused(pn, limits, query, grad, keys, values, stats, act_t, weight, row_state, col_state):
+    for wait in ledger.values():
+        wait()
+
+
+def fused(pn, limits, query, grad, keys, values, norm, delta, act, weight, row_state, col_state):
     kw, qw = pn.kv * HD, pn.kv * pn.group * HD
     whole = WINDOW + pn.tokens
     smem = pl.BlockSpec(memory_space=pltpu.SMEM)
     vmem = pl.BlockSpec(memory_space=pltpu.VMEM)
     hbm = pl.BlockSpec(memory_space=pl.ANY)
     dma = pltpu.SemaphoreType.DMA
-    half = pn.upper // pn.share
+    half = pn.half
     peers = pn.gather * pn.n_head - 1 + pn.upper - 1
     reach, gather, split = pn.reach, pn.gather, pn.split
     piece = (pn.tokens, kw) if split == gather else (pn.tok_len, kw)
@@ -541,14 +577,18 @@
             jax.ShapeDtypeStruct((pn.rows, pn.width), F32),
             jax.ShapeDtypeStruct((8, 128), F32),
         ],
-        in_specs=[smem, vmem, vmem, vmem, vmem, vmem, hbm, vmem, vmem, vmem],
+        in_specs=[smem, hbm, hbm, hbm, hbm, vmem, vmem, hbm, hbm, vmem, vmem],
         out_specs=[hbm, hbm, hbm, vmem, vmem],
         scratch_shapes=[
+            pltpu.VMEM((pn.kv_local, 2 * pn.group, pn.tok_len), F32),
+            pltpu.VMEM((pn.rows, pn.width), BF16),
+            pltpu.VMEM((pn.tok_len, pn.wide) if pn.inside else act.shape[1:], BF16),
+            pltpu.VMEM((pn.wide, pn.tok_len) if pn.inside else (16, 128), BF16),
             pltpu.VMEM((pn.tokens, qw), BF16),
             pltpu.VMEM((pn.tokens, qw), BF16),
             pltpu.VMEM((whole, kw), BF16),
             pltpu.VMEM((whole, kw), BF16),
-            pltpu.VMEM((split, pn.kv, 2 * pn.subs, pn.group * SUB), F32),
+            pltpu.VMEM((split, pn.kv, 2 * pn.group, pn.tok_len), F32),
             pltpu.VMEM((whole, kw), F32),
             pltpu.VMEM((whole, kw), F32),
             pltpu.VMEM((pn.tokens, qw), BF16),
@@ -564,10 +604,10 @@
             pltpu.VMEM((pn.streams, pn.upper - 1, pn.rows, pn.part), BF16),
             pltpu.VMEM((3, 8, 128), F32),
             pltpu.VMEM((peers, 8, 128), F32),
-            dma((5,)), dma((5, split)), dma((5, split)), dma((2, reach)), dma((2, reach)),
-            dma((2, reach)), dma((2, reach)), dma((pn.upper,)),
+            dma((7,)), dma((5, split)), dma((5, split)), dma((2, reach)), dma((2, reach)),
+            dma((2, reach)), dma((2, reach)), dma((half,)),
             dma((gather, half)), dma((gather, half)), dma((gather,)), dma((gather,)),
-            dma((gather,)), dma((gather,)), dma((split,)), dma((split,)),
+            dma((gather, 2)), dma((gather, 2)), dma((split,)), dma((split,)),
             dma((split,)), dma((split,)), dma((2 + gather,)),
             dma((pn.streams, pn.bits)), dma((pn.streams, pn.bits)), dma((peers,)), dma((peers,)),
         ],
@@ -575,7 +615,50 @@
             collective_id=0, has_side_effects=True, vmem_limit_bytes=56 * 1024 * 1024
         ),
         name="fused",
-    )(limits, query, grad, keys, values, stats, act_t, weight, row_state, col_state)
+    )(limits, query, grad, keys, values, norm, delta, act, weight, row_state, col_state)
+
+
+def finish_kernel(
+    dq_in, dk_in, dv_in, w_in, sc_in, fac_ref, dq, dk, dv, new, upd,
+    dq_v, dk_v, dv_v, w_v, sc_v, new_v, upd_v, in_sem, out_sem,
+):
+    pairs = [(dq_in, dq_v, dq), (dk_in, dk_v, dk), (dv_in, dv_v, dv)]
+    loads = [pltpu.make_async_copy(sc_in, sc_v, in_sem.at[3]), pltpu.make_async_copy(w_in, w_v, in_sem.at[4])]
+    for copy in loads:
+        copy.start()
+    ins = [pltpu.make_async_copy(a, b, in_sem.at[i]) for i, (a, b, _) in enumerate(pairs)]
+    outs = [pltpu.make_async_copy(b, d, out_sem.at[i]) for i, (_, b, d) in enumerate(pairs)]
+    outs += [pltpu.make_async_copy(new_v, new, out_sem.at[3]), pltpu.make_async_copy(upd_v, upd, out_sem.at[4])]
+    for copy in ins:
+        copy.start()
+    for copy in loads:
+        copy.wait()
+    update = sc_v[...] * fac_ref[0:1, 0:1]
+    upd_v[...] = update
+    outs[4].start()
+    new_v[...] = (w_v[...].astype(F32) - LEARN_RATE * update).astype(BF16)
+    outs[3].start()
+    for i in range(3):
+        ins[i].wait()
+        outs[i].start()
+    for copy in outs:
+        copy.wait()
+
+
+def finish(dq, dk, dv, weight, scaled, factor):
+    hbm = pl.BlockSpec(memory_space=pl.ANY)
+    vmem = pl.BlockSpec(memory_space=pltpu.VMEM)
+    arrays = [dq, dk, dv, weight, scaled]
+    outs = [dq, dk, dv, weight, scaled]
+    return pl.pallas_call(
+        finish_kernel,
+        out_shape=[jax.ShapeDtypeStruct(x.shape, x.dtype) for x in outs],
+        in_specs=[hbm] * 5 + [vmem],
+        out_specs=[hbm] * 5,
+        scratch_shapes=[pltpu.VMEM(x.shape, x.dtype) for x in arrays + [weight, scaled]]
+        + [pltpu.SemaphoreType.DMA((5,)), pltpu.SemaphoreType.DMA((5,))],
+        name="finish",
+    )(*arrays, factor)
 
 
 def shards(
@@ -588,19 +671,12 @@
     rows, width = value_weight.shape
     pn = Plan(n, n_head, tok_len, kv_local, group, width, rows)
 
-    def arranged(x):
-        x = x.reshape(pn.subs, SUB, kv_local, group)
-        return jnp.transpose(x, (2, 0, 3, 1)).reshape(kv_local, pn.subs, group * SUB)
-
-    stats = jnp.concatenate([arranged(log_norm * LOG2E), arranged(delta_rows)], axis=1)
-    act_t = activations.T.reshape(n, rows, tok_len)
+    act = activations if pn.inside else activations.T.reshape(n, rows, tok_len)
     query_grad, key_grad, value_grad, scaled, factor = fused(
-        pn, window_len, query_rows, out_grad, key_rows, value_rows, stats, act_t,
-        value_weight, row_state.reshape(-1, 1), col_state,
+        pn, window_len, query_rows, out_grad, key_rows, value_rows, log_norm.T, delta_rows.T, act,
+        value_weight, row_state, col_state,
     )
-    update_dir = scaled * factor[0, 0]
-    new_weight = (value_weight.astype(F32) - LEARN_RATE * update_dir).astype(BF16)
-    return (query_grad, key_grad, value_grad, new_weight, update_dir)
+    return finish(query_grad, key_grad, value_grad, value_weight, scaled, factor)
 
 
 def solution(mesh):

time: 122 us -> 102 us (0.84)
  local copies, waits for them, and re-layouts: 14.5 us -> 0 us
  other arithmetic: 4.17 us -> 0 us
    transpose x3 -> x0, local copies, waits for them, and re-layouts: 6.41 us -> none  [the longest x1 6.4 us: shards(): act_t = activations.T.reshape(n, rows, tok_len)]
    unnamed x7 -> x0, local copies, waits for them, and re-layouts: 4.58 us -> none
    pallas_call x1, Pallas kernels: 102 us -> 97.6 us  [fused(): pl.pallas_call(functools.partial(fused_kernel, pn), out_shape=[jax.ShapeD...]
    pallas_call x0 -> x1, Pallas kernels: none -> 3.56 us  [finish(): pl.pallas_call(finish_kernel, out_shape=[jax.ShapeDtypeStruct(x.shape, x....]
    convert_element_type x1 -> x0, other arithmetic: 2.83 us -> none  [shards(): (value_weight.astype(F32) - LEARN_RATE * update_dir).astype(BF16)]
    reshape x5 -> x0, local copies, waits for them, and re-layouts: 2.24 us -> none  [the longest x1 1.49 us: shards(): row_state.reshape(-1, 1)]
    slice x1 -> x0, local copies, waits for them, and re-layouts: 1.23 us -> none  [shards(): update_dir = scaled * factor[0, 0]]
where the time goes in v1:
time: 102 us
  Pallas kernels  101 us (99%)
    pallas_call x1, Pallas kernels, fused(): pl.pallas_call(functools.partial(fused_kernel, pn), out_shape=[jax.ShapeD...  97.6 us
    pallas_call x1, Pallas kernels, finish(): pl.pallas_call(finish_kernel, out_shape=[jax.ShapeDtypeStruct(x.shape, x....  3.56 us

profile of v1, /device:TPU:0, one launch (start us, length us, event | category | flops | bytes accessed | tf_op | source)
XLA Modules:
  0.0 101.8 jit_solution(16407954576953961986)
XLA Ops:
  0.6 97.6 %fused.1 = (bf16[384,1024]{1,0:T(8,128)(2,1)}, bf16[384,512]{1,0:T(8,128)(2,1)}, bf16[384,512]{1,0:T(8,128)(2,1)}, f32[336,512]{1,0:T(8,128)}, f32[8,128]{1,0:T(8,128)}) custom-call(s32[8]{0:T(128)} %lim_ref.1, bf16[384,1024]{1,0:T(8,128)(2,1)} %q_ref.1, bf16[384,1024]{1,0:T(8,128)(2,1)} %g_ref.1, bf16[384,512]{1,0:T(8,128)(2,1)} %k_ref.1, ...), custom_call_target="tpu_custom_call" | custom-call | tf_op jit(solution)/shard_map/fused/pallas_call | solution.py:571
  98.2 3.6 %finish.1 = (bf16[384,1024]{1,0:T(8,128)(2,1)}, bf16[384,512]{1,0:T(8,128)(2,1)}, bf16[384,512]{1,0:T(8,128)(2,1)}, bf16[336,512]{1,0:T(8,128)(2,1)}, f32[336,512]{1,0:T(8,128)}) custom-call(bf16[384,1024]{1,0:T(8,128)(2,1)} %get-tuple-element.10.dq_in, bf16[384,512]{1,0:T(8,128)(2,1)} %get-tuple-element.11.dk_in, bf16[384,512]{1,0:T(8,128)(2,1)} %get-tuple-element.12.dv_in, ...), custom_call_target="tpu_custom_call" | custom-call | tf_op jit(solution)/shard_map/finish/pallas_call | solution.py:653

commit v2 on v1

--- a/solution.py
+++ b/solution.py
@@ -50,6 +50,10 @@
         self.half = self.upper // self.share
         self.wide = self.half * self.gather * rows
         self.inside = rows % 16 == 0 and self.wide % SUB == 0
+        first = rows * 5 // 6 // 16 * 16
+        cut = self.inside and self.split == self.gather and first
+        self.parts = [(0, first), (first, rows - first)] if cut else [(0, rows)]
+        self.flat = n * n_head <= 64
 
     def halo_count(self, o):
         return min(self.tokens, WINDOW - (o - 1) * self.tokens)
@@ -85,11 +89,11 @@
 
 def fused_kernel(
     pn,
-    lim_ref, q_ref, g_ref, k_ref, v_ref, ln_ref, de_ref, at_ref, w_ref, rs_ref, cs_ref,
-    dq_ref, dk_ref, dv_ref, sc_ref, fac_ref,
-    st, wv, abuf, turned, qb, gb, kb, vb, stb, dva, dka, dqb, dkb, hsv, hsk, hrv, hrk, act, vga, acc, sbuf, rbuf,
+    lim_in, q_ref, g_ref, k_ref, v_ref, ln_in, de_in, at_ref, w_ref, rs_in, cs_in,
+    dq_ref, dk_ref, dv_ref, sc_out, fac_out,
+    lim_ref, ln_ref, de_ref, rs_ref, cs_ref, sc_ref, fac_ref, st, wv, abuf, turned, qb, gb, kb, vb, stb, dva, dka, dqb, dkb, hsv, hsk, hrv, hrk, act, vga, acc, sbuf, rbuf,
     xs, xr,
-    own_sem, in_s, in_r, halo_s, halo_r, back_s, back_r, act_own, act_s, act_r, fwd_s, fwd_r,
+    own_sem, small_sem, in_s, in_r, halo_s, halo_r, back_s, back_r, act_own, act_s, act_r, fwd_s, fwd_r,
     vg_s, vg_r, dq_s, dq_r, dk_s, dk_r, out_sem, rs_s, rs_r, x_s, x_r,
 ):
     n, n_head, gather, upper = pn.n, pn.n_head, pn.gather, pn.upper
@@ -143,6 +147,13 @@
         load.start()
     for copy in own[:4]:
         copy.start()
+    small = [
+        pltpu.make_async_copy(src, dst, small_sem.at[i])
+        for i, (src, dst) in enumerate(
+            [(ln_in, ln_ref), (de_in, de_ref), (lim_in, lim_ref), (rs_in, rs_ref), (cs_in, cs_ref)])
+    ]
+    for copy in small:
+        copy.start()
     weight_in = pltpu.make_async_copy(w_ref, wv, own_sem.at[6])
     weight_in.start()
 
@@ -170,6 +181,8 @@
     for a in (0, 1, 2, 3):
         for j in range(1, split):
             exchange(a, j).start()
+    for copy in small:
+        copy.wait()
     for i, ref in enumerate((ln_ref, de_ref)):
         stat = ref[...]
         if i == 0:
@@ -221,31 +234,56 @@
     if pn.inside:
         turn(0, steps)
 
-    def act_piece(i, owner):
+    parts = pn.parts
+
+    def act_piece(i, owner, r):
+        first, size = parts[r]
         if pn.inside:
-            return turned.at[pl.ds(pl.multiple_of((i * gather + owner) * rows, 16), rows)]
+            here = pl.multiple_of((i * gather + owner) * rows + first, 16)
+            return turned.at[pl.ds(here, size)]
         return at_ref.at[(low + i) * gather + owner]
 
     act_mine = [
-        pltpu.make_async_copy(act_piece(i, c), act.at[low + i, :, cols(c, length)], act_own.at[i])
-        for i in range(half)
+        pltpu.make_async_copy(
+            act_piece(i, c, r), act.at[low + i, pl.ds(*parts[r]), cols(c, length)], act_own.at[i, r])
+        for i in range(half) for r in range(len(parts))
     ]
     for copy in act_mine:
         copy.start()
 
-    def act_send(j, i):
+    def act_send(j, i, r):
         return Link(
-            ledger, ("act", j, i), act_piece(i, xor(c, j)), act.at[low + i, :, cols(c, length)],
-            (act_s, act_r), (j, i), at_plane(j),
-        )
-
-    def act_forward(j):
-        piece = act.at[pl.ds(low, half), :, cols(xor(c, j), length)]
-        return Link(ledger, ("forward", j), piece, piece, (fwd_s, fwd_r), (j,), {"head": xor(hd, 1)})
-
-    for i in range(half):
-        for j in range(1, gather):
-            act_send(j, i).start()
+            ledger, ("act", j, i, r), act_piece(i, xor(c, j), r),
+            act.at[low + i, pl.ds(*parts[r]), cols(c, length)],
+            (act_s, act_r), (j, i, r), at_plane(j),
+        )
+
+    def act_forward(j, i, r, start=low):
+        piece = act.at[start + i, pl.ds(*parts[r]), cols(xor(c, j), length)]
+        return Link(
+            ledger, ("forward", j, i, r), piece, piece, (fwd_s, fwd_r), (j, i, r),
+            {"head": xor(hd, 1)})
+
+    order = [(j, i) for i in range(half) for j in (1, 2, 3)]
+    if gather == 1:
+        order = []
+
+    def act_out(r):
+        for j, i in order:
+            act_send(j, i, r).start()
+
+    def act_pass(r):
+        for j, i in order:
+            act_send(j, i, r).wait_recv()
+            if pn.share == 2:
+                act_forward(j, i, r).start()
+
+    def act_ready(r):
+        if pn.share == 2:
+            for j, i in [(0, i) for i in range(half)] + order:
+                act_forward(j, i, r, half - low).wait_recv()
+
+    act_out(0)
     for a in (0, 1):
         for o in range(1, pn.reach + 1):
             halo(a, o).wait_recv()
@@ -340,7 +378,9 @@
             for copy in act_mine:
                 copy.wait()
             if pn.share == 2:
-                act_forward(0).start()
+                for r in range(len(parts)):
+                    for i in range(half):
+                        act_forward(0, i, r).start()
 
     def back(a, o):
         count, first = pn.halo_count(o), pn.halo_first(o)
@@ -381,26 +421,14 @@
     def vg_wait(j, h):
         vg_copy(j, xor(c, j), h).wait_recv()
 
+    act_pass(0)
     add_back(0)
     vga[c] = dva[pl.ds(WINDOW, tokens)].astype(BF16)
     if gather > 1:
         for h in (0, 1):
             vg_send(1, h).start()
             vg_send(2, 1 - h).start()
-    for j in range(1, gather):
-        for i in range(half):
-            act_send(j, i).wait_recv()
-        if pn.share == 2:
-            act_forward(j).start()
-
-    if pn.share == 2:
-        for j in range(gather):
-            piece_in = act.at[pl.ds(half - low, half), :, cols(xor(c, j), length)]
-            Link(
-                ledger, ("forward", j), piece_in, piece_in, (fwd_s, fwd_r), (j,),
-                {"head": xor(hd, 1)},
-            ).wait_recv()
-
+    act_ready(0)
     bits, part = pn.bits, pn.part
     counts = [upper >> (p + 1) for p in range(bits)]
     starts = [sum(counts[:p]) for p in range(bits)]
@@ -417,16 +445,50 @@
         index = index + (1 << phase) * ((1 - mine) if other else mine)
         return index + (1 << (phase + 1)) * j
 
-    def copy_of(s, p):
-        here = pl.ds(starts[p], counts[p])
+    def copy_of(s, p, r):
+        here, there = pl.ds(starts[p], counts[p]), pl.ds(*parts[r])
         return Link(
-            ledger, ("sum", s, p), sbuf.at[s, here], rbuf.at[s, here], (rs_s, rs_r), (s, p), partners[p])
-
-    def product(s, index):
+            ledger, ("sum", s, p, r), sbuf.at[s, here, there], rbuf.at[s, here, there],
+            (rs_s, rs_r), (s, p, r), partners[p],
+        )
+
+    def product(s, index, r):
+        left = act[index, pl.ds(*parts[r]), :]
         if split == gather:
-            return jnp.dot(act[index], vga[xor(c, s)], preferred_element_type=F32)
+            return jnp.dot(left, vga[xor(c, s)], preferred_element_type=F32)
         whole = vga[...].reshape(gather * length, part)
-        return jnp.dot(act[index], whole, preferred_element_type=F32)
+        return jnp.dot(left, whole, preferred_element_type=F32)
+
+    def products(s, r):
+        there = pl.ds(*parts[r])
+
+        @pl.loop(0, counts[0])
+        def _(j):
+            sbuf[s, j, there] = product(s, block_at(0, j, True), r).astype(BF16)
+
+        copy_of(s, 0, r).start()
+
+        @pl.loop(0, counts[0])
+        def _(j):
+            index = block_at(0, j, False)
+            acc[s, index, there] = product(s, index, r)
+
+    def arrived(s, p, r):
+        there = pl.ds(*parts[r])
+        copy_of(s, p, r).wait_recv()
+
+        @pl.loop(0, counts[p])
+        def _(j):
+            index = block_at(p, j, False)
+            acc[s, index, there] = acc[s, index, there] + rbuf[s, starts[p] + j, there].astype(F32)
+
+        if p + 1 < bits:
+            @pl.loop(0, counts[p + 1])
+            def _(j):
+                index = block_at(p + 1, j, True)
+                sbuf[s, starts[p + 1] + j, there] = acc[s, index, there].astype(BF16)
+
+            copy_of(s, p + 1, r).start()
 
     def pass_on():
         vg_wait(1, 0)
@@ -434,31 +496,22 @@
         vg_wait(2, 1)
         vg_send(3, 1).start()
 
+    last = len(parts) - 1
     if split == 1 and gather > 1:
         pass_on()
         vg_wait(1, 1)
         vg_wait(2, 0)
         vg_wait(3, 0)
         vg_wait(3, 1)
-    for s in range(pn.streams):
-        if s == 1:
-            pass_on()
-        if s == 3:
-            vg_wait(3, 0)
-            vg_wait(3, 1)
-        elif s:
+    products(0, 0)
+    if split > 1:
+        pass_on()
+        if last:
+            act_out(1)
+            arrived(0, 0, 0)
+        for s in (1, 2):
             vg_wait(s, s % 2)
-
-        @pl.loop(0, counts[0])
-        def _(j, s=s):
-            sbuf[s, j] = product(s, block_at(0, j, True)).astype(BF16)
-
-        copy_of(s, 0).start()
-
-        @pl.loop(0, counts[0])
-        def _(j, s=s):
-            index = block_at(0, j, False)
-            acc[s, index] = product(s, index)
+            products(s, 0)
 
     outs = []
     outs.append(local_out(dqb.at[pl.ds(place * length, length)], dq_ref.at[:, cols(place, qw)], 0))
@@ -480,6 +533,20 @@
     outs[-1].start()
     for j in range(1, split):
         dk_send(j).start()
+    if last:
+        vg_wait(3, 0)
+        vg_wait(3, 1)
+        products(3, 0)
+        arrived(1, 0, 0)
+        arrived(2, 0, 0)
+        act_pass(1)
+        act_ready(1)
+        for s in range(4):
+            products(s, 1)
+    elif split > 1:
+        vg_wait(3, 0)
+        vg_wait(3, 1)
+        products(3, 0)
     if split == gather:
         for j in range(gather):
             src = xor(c, j)
@@ -494,22 +561,16 @@
     weight_f = wv[...].astype(F32)
     weight_sum = jnp.sum(weight_f * weight_f)
 
-    for p in range(bits):
-        for s in range(pn.streams):
-            copy_of(s, p).wait_recv()
-
-            @pl.loop(0, counts[p])
-            def _(j, s=s, p=p):
-                index = block_at(p, j, False)
-                acc[s, index] = acc[s, index] + rbuf[s, starts[p] + j].astype(F32)
-
-            if p + 1 < bits:
-                @pl.loop(0, counts[p + 1])
-                def _(j, s=s, p=p):
-                    index = block_at(p + 1, j, True)
-                    sbuf[s, starts[p + 1] + j] = acc[s, index].astype(BF16)
-
-                copy_of(s, p + 1).start()
+    early, late = list(range(min(3, pn.streams))), list(range(3, pn.streams))
+    steps = [(s, 0, last) for s in early]
+    if last:
+        steps += [(s, 1, 0) for s in early] if bits > 1 else []
+    steps = ([(s, 0, 0) for s in late] if last else []) + steps + [(s, 0, last) for s in late]
+    for p in range(1, bits):
+        steps += [(s, p, r) for r in range(len(parts)) for s in early if p > 1 or r == last]
+        steps += [(s, p, r) for r in range(len(parts)) for s in late]
+    for s, p, r in steps:
+        arrived(s, p, r)
 
     row_sum = jnp.zeros((rows, 1), F32)
     for s in range(pn.streams):
@@ -530,14 +591,24 @@
         sc_ref[:, here] = scaled
         scaled_sum = scaled_sum + jnp.sum(scaled * scaled)
 
+    outs.append(local_out(sc_ref, sc_out, 2 + gather))
+    outs[-1].start()
     row = lax.broadcasted_iota(jnp.int32, (8, 128), 0)
     xs[0] = jnp.where(row < 4, scaled_sum, weight_sum)
+
+    if pn.flat:
+        levels = [[
+            {"tok": xor(u, i) * gather + xor(c, j), "head": xor(hd, h)}
+            for i in range(upper) for j in range(gather) for h in range(n_head) if i or j or h
+        ]]
+    else:
+        levels = [near_ids, far_ids]
 
     def share(level, i, partner):
         slot = i + (len(near) if level else 0)
         return Link(ledger, ("share", slot), xs.at[level], xr.at[slot], (x_s, x_r), (slot,), partner)
 
-    for level, ids in enumerate((near_ids, far_ids)):
+    for level, ids in enumerate(levels):
         for i, partner in enumerate(ids):
             share(level, i, partner).start()
         total = xs[level]
@@ -545,12 +616,14 @@
             share(level, i, partner).wait_recv()
             total = total + xr[i + (len(near) if level else 0)]
         xs[level + 1] = total
-    sums = xs[2]
+    sums = xs[len(levels)]
     size = float(rows * n * pn.width * n_head)
     rms_scaled = jnp.sqrt(sums[0:1] / size)
     rms_weight = jnp.sqrt(sums[4:5] / size)
     fac_ref[...] = jnp.broadcast_to(rms_weight / jnp.maximum(1.0, rms_scaled), fac_ref.shape)
 
+    outs.append(local_out(fac_ref, fac_out, 3 + gather))
+    outs[-1].start()
     for copy in outs:
         copy.wait()
     for wait in ledger.values():
@@ -560,12 +633,10 @@
 def fused(pn, limits, query, grad, keys, values, norm, delta, act, weight, row_state, col_state):
     kw, qw = pn.kv * HD, pn.kv * pn.group * HD
     whole = WINDOW + pn.tokens
-    smem = pl.BlockSpec(memory_space=pltpu.SMEM)
-    vmem = pl.BlockSpec(memory_space=pltpu.VMEM)
     hbm = pl.BlockSpec(memory_space=pl.ANY)
     dma = pltpu.SemaphoreType.DMA
-    half = pn.half
-    peers = pn.gather * pn.n_head - 1 + pn.upper - 1
+    half, cuts = pn.half, len(pn.parts)
+    peers = pn.n * pn.n_head - 1 if pn.flat else pn.gather * pn.n_head - 1 + pn.upper - 1
     reach, gather, split = pn.reach, pn.gather, pn.split
     piece = (pn.tokens, kw) if split == gather else (pn.tok_len, kw)
     return pl.pallas_call(
@@ -577,9 +648,16 @@
             jax.ShapeDtypeStruct((pn.rows, pn.width), F32),
             jax.ShapeDtypeStruct((8, 128), F32),
         ],
-        in_specs=[smem, hbm, hbm, hbm, hbm, vmem, vmem, hbm, hbm, vmem, vmem],
-        out_specs=[hbm, hbm, hbm, vmem, vmem],
+        in_specs=[hbm] * 11,
+        out_specs=[hbm] * 5,
         scratch_shapes=[
+            pltpu.SMEM(limits.shape, jnp.int32),
+            pltpu.VMEM(norm.shape, F32),
+            pltpu.VMEM(delta.shape, F32),
+            pltpu.VMEM(row_state.shape, F32),
+            pltpu.VMEM(col_state.shape, F32),
+            pltpu.VMEM((pn.rows, pn.width), F32),
+            pltpu.VMEM((8, 128), F32),
             pltpu.VMEM((pn.kv_local, 2 * pn.group, pn.tok_len), F32),
             pltpu.VMEM((pn.rows, pn.width), BF16),
             pltpu.VMEM((pn.tok_len, pn.wide) if pn.inside else act.shape[1:], BF16),
@@ -604,12 +682,13 @@
             pltpu.VMEM((pn.streams, pn.upper - 1, pn.rows, pn.part), BF16),
             pltpu.VMEM((3, 8, 128), F32),
             pltpu.VMEM((peers, 8, 128), F32),
-            dma((7,)), dma((5, split)), dma((5, split)), dma((2, reach)), dma((2, reach)),
-            dma((2, reach)), dma((2, reach)), dma((half,)),
-            dma((gather, half)), dma((gather, half)), dma((gather,)), dma((gather,)),
+            dma((7,)), dma((5,)), dma((5, split)), dma((5, split)), dma((2, reach)), dma((2, reach)),
+            dma((2, reach)), dma((2, reach)), dma((half, cuts)),
+            dma((gather, half, cuts)), dma((gather, half, cuts)),
+            dma((gather, half, cuts)), dma((gather, half, cuts)),
             dma((gather, 2)), dma((gather, 2)), dma((split,)), dma((split,)),
-            dma((split,)), dma((split,)), dma((2 + gather,)),
-            dma((pn.streams, pn.bits)), dma((pn.streams, pn.bits)), dma((peers,)), dma((peers,)),
+            dma((split,)), dma((split,)), dma((4 + gather,)),
+            dma((pn.streams, pn.bits, cuts)), dma((pn.streams, pn.bits, cuts)), dma((peers,)), dma((peers,)),
         ],
         compiler_params=pltpu.CompilerParams(
             collective_id=0, has_side_effects=True, vmem_limit_bytes=56 * 1024 * 1024
@@ -619,11 +698,11 @@
 
 
 def finish_kernel(
-    dq_in, dk_in, dv_in, w_in, sc_in, fac_ref, dq, dk, dv, new, upd,
-    dq_v, dk_v, dv_v, w_v, sc_v, new_v, upd_v, in_sem, out_sem,
+    dq_in, dk_in, dv_in, w_in, sc_in, fac_in, dq, dk, dv, new, upd,
+    dq_v, dk_v, dv_v, w_v, sc_v, new_v, upd_v, fac_ref, in_sem, out_sem,
 ):
     pairs = [(dq_in, dq_v, dq), (dk_in, dk_v, dk), (dv_in, dv_v, dv)]
-    loads = [pltpu.make_async_copy(sc_in, sc_v, in_sem.at[3]), pltpu.make_async_copy(w_in, w_v, in_sem.at[4])]
+    loads = [pltpu.make_async_copy(fac_in, fac_ref, in_sem.at[5]), pltpu.make_async_copy(sc_in, sc_v, in_sem.at[3]), pltpu.make_async_copy(w_in, w_v, in_sem.at[4])]
     for copy in loads:
         copy.start()
     ins = [pltpu.make_async_copy(a, b, in_sem.at[i]) for i, (a, b, _) in enumerate(pairs)]
@@ -647,16 +726,15 @@
 
 def finish(dq, dk, dv, weight, scaled, factor):
     hbm = pl.BlockSpec(memory_space=pl.ANY)
-    vmem = pl.BlockSpec(memory_space=pltpu.VMEM)
     arrays = [dq, dk, dv, weight, scaled]
     outs = [dq, dk, dv, weight, scaled]
     return pl.pallas_call(
         finish_kernel,
         out_shape=[jax.ShapeDtypeStruct(x.shape, x.dtype) for x in outs],
-        in_specs=[hbm] * 5 + [vmem],
+        in_specs=[hbm] * 6,
         out_specs=[hbm] * 5,
-        scratch_shapes=[pltpu.VMEM(x.shape, x.dtype) for x in arrays + [weight, scaled]]
-        + [pltpu.SemaphoreType.DMA((5,)), pltpu.SemaphoreType.DMA((5,))],
+        scratch_shapes=[pltpu.VMEM(x.shape, x.dtype) for x in arrays + [weight, scaled, factor]]
+        + [pltpu.SemaphoreType.DMA((6,)), pltpu.SemaphoreType.DMA((5,))],
         name="finish",
     )(*arrays, factor)
 

time: 102 us -> 97.5 us (0.956)
  Pallas kernels: 101 us -> 96.7 us
    pallas_call x1, Pallas kernels: 97.6 us -> 93.8 us  [fused(): pl.pallas_call(functools.partial(fused_kernel, pn), out_shape=[jax.ShapeD...]
where the time goes in v2:
time: 97.5 us; the launch traced here: 97.3 us
  Pallas kernels  96.7 us (99%)
    pallas_call x1, Pallas kernels, fused(): pl.pallas_call(functools.partial(fused_kernel, pn), out_shape=[jax.ShapeD...  93.8 us
    pallas_call x1, Pallas kernels, finish(): pl.pallas_call(finish_kernel, out_shape=[jax.ShapeDtypeStruct(x.shape, x....  2.9 us

profile of v2, /device:TPU:0, one launch (start us, length us, event | category | flops | bytes accessed | tf_op | source)
XLA Modules:
  0.0 97.3 jit_solution(10516677675683604303)
XLA Ops:
  0.6 93.8 %fused.1 = (bf16[384,1024]{1,0:T(8,128)(2,1)}, bf16[384,512]{1,0:T(8,128)(2,1)}, bf16[384,512]{1,0:T(8,128)(2,1)}, f32[336,512]{1,0:T(8,128)}, f32[8,128]{1,0:T(8,128)}) custom-call(s32[8]{0:T(128)} %lim_in.1, bf16[384,1024]{1,0:T(8,128)(2,1)} %q_ref.1, bf16[384,1024]{1,0:T(8,128)(2,1)} %g_ref.1, bf16[384,512]{1,0:T(8,128)(2,1)} %k_ref.1, ...), custom_call_target="tpu_custom_call" | custom-call | tf_op jit(solution)/shard_map/fused/pallas_call | solution.py:642
  94.4 2.9 %finish.1 = (bf16[384,1024]{1,0:T(8,128)(2,1)}, bf16[384,512]{1,0:T(8,128)(2,1)}, bf16[384,512]{1,0:T(8,128)(2,1)}, bf16[336,512]{1,0:T(8,128)(2,1)}, f32[336,512]{1,0:T(8,128)}) custom-call(bf16[384,1024]{1,0:T(8,128)(2,1)} %get-tuple-element.10.dq_in, bf16[384,512]{1,0:T(8,128)(2,1)} %get-tuple-element.11.dk_in, bf16[384,512]{1,0:T(8,128)(2,1)} %get-tuple-element.12.dv_in, ...), custom_call_target="tpu_custom_call" | custom-call | tf_op jit(solution)/shard_map/finish/pallas_call | solution.py:731

commit v3 on v2

--- a/solution.py
+++ b/solution.py
@@ -50,10 +50,18 @@
         self.half = self.upper // self.share
         self.wide = self.half * self.gather * rows
         self.inside = rows % 16 == 0 and self.wide % SUB == 0
-        first = rows * 5 // 6 // 16 * 16
+        first = rows * 5 // 7 // 16 * 16
         cut = self.inside and self.split == self.gather and first
         self.parts = [(0, first), (first, rows - first)] if cut else [(0, rows)]
         self.flat = n * n_head <= 64
+        length = self.tokens if self.split == self.gather else tok_len
+        first, middle = self.tokens - WINDOW, length // 2
+        self.ahead = self.split == self.gather and 0 < first < middle and first % 16 == 0
+        if self.ahead:
+            self.pieces = [(0, first), (first, middle - first), (middle, length - middle)]
+        else:
+            self.pieces = [(0, middle), (middle, length - middle)]
+        self.tail = len(self.pieces) - 1
 
     def halo_count(self, o):
         return min(self.tokens, WINDOW - (o - 1) * self.tokens)
@@ -390,10 +398,30 @@
             {"tok": me - o * split}, block >= o, block + o < pn.blocks,
         )
 
+    tail = pn.tail
+
+    def vg_copy(j, owner, h):
+        piece = vga.at[owner, pl.ds(*pn.pieces[h])]
+        return Link(
+            ledger, ("vg", j, h), piece, piece, (vg_s, vg_r), (j, h),
+            at_plane(j if j < 3 else (1 if h == tail else 2)),
+        )
+
+    def vg_send(j, h):
+        return vg_copy(j, c if j < 3 else xor(c, 2 if h == tail else 1), h)
+
+    def vg_wait(j, h):
+        vg_copy(j, xor(c, j), h).wait_recv()
+
     for a in (0, 1):
         (hsv, hsk)[a][...] = (dva, dka)[a][pl.ds(0, WINDOW)].astype(BF16)
         for o in range(1, pn.reach + 1):
             back(a, o).start()
+        if a == 0 and pn.ahead:
+            first = pn.pieces[0][1]
+            vga[c, pl.ds(0, first)] = dva[pl.ds(WINDOW, first)].astype(BF16)
+            for j in (1, 2):
+                vg_send(j, 0).start()
 
     def add_back(a):
         for o in range(1, pn.reach + 1):
@@ -406,28 +434,15 @@
                 total = (dva, dka)[a]
                 total[here] = total[here] + (hrv, hrk)[a][o - 1, pl.ds(0, count)].astype(F32)
 
-    cut = vga.shape[1] // 2
-
-    def vg_copy(j, owner, part_of):
-        piece = vga.at[owner, pl.ds(part_of * cut, cut)]
-        return Link(
-            ledger, ("vg", j, part_of), piece, piece, (vg_s, vg_r), (j, part_of),
-            at_plane(j if j < 3 else (2, 1)[part_of]),
-        )
-
-    def vg_send(j, h):
-        return vg_copy(j, c if j < 3 else xor(c, (1, 2)[h]), h)
-
-    def vg_wait(j, h):
-        vg_copy(j, xor(c, j), h).wait_recv()
-
     act_pass(0)
     add_back(0)
-    vga[c] = dva[pl.ds(WINDOW, tokens)].astype(BF16)
+    ready = pn.pieces[0][1] if pn.ahead else 0
+    vga[c, pl.ds(ready, tokens - ready)] = dva[pl.ds(WINDOW + ready, tokens - ready)].astype(BF16)
+    rest = list(range(1 if pn.ahead else 0, len(pn.pieces)))
     if gather > 1:
-        for h in (0, 1):
+        for h, g in zip(rest, rest[::-1]):
             vg_send(1, h).start()
-            vg_send(2, 1 - h).start()
+            vg_send(2, g).start()
     act_ready(0)
     bits, part = pn.bits, pn.part
     counts = [upper >> (p + 1) for p in range(bits)]
@@ -491,18 +506,24 @@
             copy_of(s, p + 1, r).start()
 
     def pass_on():
-        vg_wait(1, 0)
-        vg_send(3, 0).start()
-        vg_wait(2, 1)
-        vg_send(3, 1).start()
+        for h in range(tail - 1):
+            vg_wait(1, h)
+            vg_send(3, h).start()
+        vg_wait(2, tail)
+        vg_send(3, tail).start()
+        vg_wait(1, tail - 1)
+        vg_send(3, tail - 1).start()
+
+    def vg_rest(j):
+        for h in range(tail + 1):
+            if j == 3 or (j == 1 and h == tail) or (j == 2 and h != tail):
+                vg_wait(j, h)
 
     last = len(parts) - 1
     if split == 1 and gather > 1:
         pass_on()
-        vg_wait(1, 1)
-        vg_wait(2, 0)
-        vg_wait(3, 0)
-        vg_wait(3, 1)
+        for j in (1, 2, 3):
+            vg_rest(j)
     products(0, 0)
     if split > 1:
         pass_on()
@@ -510,14 +531,12 @@
             act_out(1)
             arrived(0, 0, 0)
         for s in (1, 2):
-            vg_wait(s, s % 2)
+            vg_rest(s)
             products(s, 0)
 
     outs = []
     outs.append(local_out(dqb.at[pl.ds(place * length, length)], dq_ref.at[:, cols(place, qw)], 0))
     outs[-1].start()
-    for j in range(1, split):
-        dq_send(j).start()
 
     add_back(1)
     dkb[...] = dka[pl.ds(WINDOW, tokens)].astype(BF16)
@@ -531,11 +550,8 @@
 
     outs.append(local_out(dkb.at[pl.ds(place * length, length)], dk_ref.at[:, cols(place, kw)], 1))
     outs[-1].start()
-    for j in range(1, split):
-        dk_send(j).start()
     if last:
-        vg_wait(3, 0)
-        vg_wait(3, 1)
+        vg_rest(3)
         products(3, 0)
         arrived(1, 0, 0)
         arrived(2, 0, 0)
@@ -544,9 +560,12 @@
         for s in range(4):
             products(s, 1)
     elif split > 1:
-        vg_wait(3, 0)
-        vg_wait(3, 1)
+        vg_rest(3)
         products(3, 0)
+    for j in range(1, split):
+        dq_send(j).start()
+    for j in range(1, split):
+        dk_send(j).start()
     if split == gather:
         for j in range(gather):
             src = xor(c, j)
@@ -686,7 +705,7 @@
             dma((2, reach)), dma((2, reach)), dma((half, cuts)),
             dma((gather, half, cuts)), dma((gather, half, cuts)),
             dma((gather, half, cuts)), dma((gather, half, cuts)),
-            dma((gather, 2)), dma((gather, 2)), dma((split,)), dma((split,)),
+            dma((gather, len(pn.pieces))), dma((gather, len(pn.pieces))), dma((split,)), dma((split,)),
             dma((split,)), dma((split,)), dma((4 + gather,)),
             dma((pn.streams, pn.bits, cuts)), dma((pn.streams, pn.bits, cuts)), dma((peers,)), dma((peers,)),
         ],

time: 97.5 us -> 96.3 us (0.988)
  Pallas kernels: 96.7 us -> 95.5 us
    pallas_call x1, Pallas kernels: 93.8 us -> 92.6 us  [fused(): pl.pallas_call(functools.partial(fused_kernel, pn), out_shape=[jax.ShapeD...]
where the time goes in v3:
time: 96.3 us; the launch traced here: 96.1 us
  Pallas kernels  95.5 us (99%)
    pallas_call x1, Pallas kernels, fused(): pl.pallas_call(functools.partial(fused_kernel, pn), out_shape=[jax.ShapeD...  92.6 us
    pallas_call x1, Pallas kernels, finish(): pl.pallas_call(finish_kernel, out_shape=[jax.ShapeDtypeStruct(x.shape, x....  2.9 us

profile of v3, /device:TPU:0, one launch (start us, length us, event | category | flops | bytes accessed | tf_op | source)
XLA Modules:
  0.0 96.1 jit_solution(18283935623107387490)
XLA Ops:
  0.6 92.6 %fused.1 = (bf16[384,1024]{1,0:T(8,128)(2,1)}, bf16[384,512]{1,0:T(8,128)(2,1)}, bf16[384,512]{1,0:T(8,128)(2,1)}, f32[336,512]{1,0:T(8,128)}, f32[8,128]{1,0:T(8,128)}) custom-call(s32[8]{0:T(128)} %lim_in.1, bf16[384,1024]{1,0:T(8,128)(2,1)} %q_ref.1, bf16[384,1024]{1,0:T(8,128)(2,1)} %g_ref.1, bf16[384,512]{1,0:T(8,128)(2,1)} %k_ref.1, ...), custom_call_target="tpu_custom_call" | custom-call | tf_op jit(solution)/shard_map/fused/pallas_call | solution.py:661
  93.2 2.9 %finish.1 = (bf16[384,1024]{1,0:T(8,128)(2,1)}, bf16[384,512]{1,0:T(8,128)(2,1)}, bf16[384,512]{1,0:T(8,128)(2,1)}, bf16[336,512]{1,0:T(8,128)(2,1)}, f32[336,512]{1,0:T(8,128)}) custom-call(bf16[384,1024]{1,0:T(8,128)(2,1)} %get-tuple-element.10.dq_in, bf16[384,512]{1,0:T(8,128)(2,1)} %get-tuple-element.11.dk_in, bf16[384,512]{1,0:T(8,128)(2,1)} %get-tuple-element.12.dv_in, ...), custom_call_target="tpu_custom_call" | custom-call | tf_op jit(solution)/shard_map/finish/pallas_call | solution.py:750

commit v4 on v3

--- a/solution.py
+++ b/solution.py
@@ -559,13 +559,16 @@
         act_ready(1)
         for s in range(4):
             products(s, 1)
+            if s:
+                dq_send(s).start()
+                dk_send(s).start()
     elif split > 1:
         vg_rest(3)
         products(3, 0)
-    for j in range(1, split):
-        dq_send(j).start()
-    for j in range(1, split):
-        dk_send(j).start()
+    if not last:
+        for j in range(1, split):
+            dq_send(j).start()
+            dk_send(j).start()
     if split == gather:
         for j in range(gather):
             src = xor(c, j)
@@ -613,7 +616,7 @@
     outs.append(local_out(sc_ref, sc_out, 2 + gather))
     outs[-1].start()
     row = lax.broadcasted_iota(jnp.int32, (8, 128), 0)
-    xs[0] = jnp.where(row < 4, scaled_sum, weight_sum)
+    xs[0] = jnp.where(row < 1, scaled_sum, weight_sum)
 
     if pn.flat:
         levels = [[
@@ -625,20 +628,20 @@
 
     def share(level, i, partner):
         slot = i + (len(near) if level else 0)
-        return Link(ledger, ("share", slot), xs.at[level], xr.at[slot], (x_s, x_r), (slot,), partner)
+        return Link(ledger, ("share", slot), xs.at[level, pl.ds(0, 2)], xr.at[slot, pl.ds(0, 2)], (x_s, x_r), (slot,), partner)
 
     for level, ids in enumerate(levels):
         for i, partner in enumerate(ids):
             share(level, i, partner).start()
-        total = xs[level]
+        total = xs[level, pl.ds(0, 2)]
         for i, partner in enumerate(ids):
             share(level, i, partner).wait_recv()
-            total = total + xr[i + (len(near) if level else 0)]
-        xs[level + 1] = total
+            total = total + xr[i + (len(near) if level else 0), pl.ds(0, 2)]
+        xs[level + 1, pl.ds(0, 2)] = total
     sums = xs[len(levels)]
     size = float(rows * n * pn.width * n_head)
     rms_scaled = jnp.sqrt(sums[0:1] / size)
-    rms_weight = jnp.sqrt(sums[4:5] / size)
+    rms_weight = jnp.sqrt(sums[1:2] / size)
     fac_ref[...] = jnp.broadcast_to(rms_weight / jnp.maximum(1.0, rms_scaled), fac_ref.shape)
 
     outs.append(local_out(fac_ref, fac_out, 3 + gather))

time: 96.3 us -> 94.2 us (0.978)
  Pallas kernels: 95.5 us -> 93.4 us
    pallas_call x1, Pallas kernels: 92.6 us -> 90.5 us  [fused(): pl.pallas_call(functools.partial(fused_kernel, pn), out_shape=[jax.ShapeD...]
where the time goes in v4:
time: 94.2 us; the launch traced here: 94 us
  Pallas kernels  93.4 us (99%)
    pallas_call x1, Pallas kernels, fused(): pl.pallas_call(functools.partial(fused_kernel, pn), out_shape=[jax.ShapeD...  90.5 us
    pallas_call x1, Pallas kernels, finish(): pl.pallas_call(finish_kernel, out_shape=[jax.ShapeDtypeStruct(x.shape, x....  2.9 us

profile of v4, /device:TPU:0, one launch (start us, length us, event | category | flops | bytes accessed | tf_op | source)
XLA Modules:
  0.0 94.0 jit_solution(5935368998675463586)
XLA Ops:
  0.6 90.5 %fused.1 = (bf16[384,1024]{1,0:T(8,128)(2,1)}, bf16[384,512]{1,0:T(8,128)(2,1)}, bf16[384,512]{1,0:T(8,128)(2,1)}, f32[336,512]{1,0:T(8,128)}, f32[8,128]{1,0:T(8,128)}) custom-call(s32[8]{0:T(128)} %lim_in.1, bf16[384,1024]{1,0:T(8,128)(2,1)} %q_ref.1, bf16[384,1024]{1,0:T(8,128)(2,1)} %g_ref.1, bf16[384,512]{1,0:T(8,128)(2,1)} %k_ref.1, ...), custom_call_target="tpu_custom_call" | custom-call | tf_op jit(solution)/shard_map/fused/pallas_call | solution.py:664
  91.1 2.9 %finish.1 = (bf16[384,1024]{1,0:T(8,128)(2,1)}, bf16[384,512]{1,0:T(8,128)(2,1)}, bf16[384,512]{1,0:T(8,128)(2,1)}, bf16[336,512]{1,0:T(8,128)(2,1)}, f32[336,512]{1,0:T(8,128)}) custom-call(bf16[384,1024]{1,0:T(8,128)(2,1)} %get-tuple-element.10.dq_in, bf16[384,512]{1,0:T(8,128)(2,1)} %get-tuple-element.11.dk_in, bf16[384,512]{1,0:T(8,128)(2,1)} %get-tuple-element.12.dv_in, ...), custom_call_target="tpu_custom_call" | custom-call | tf_op jit(solution)/shard_map/finish/pallas_call | solution.py:753

commit v5 on v4

--- a/solution.py
+++ b/solution.py
@@ -558,10 +558,10 @@
         act_pass(1)
         act_ready(1)
         for s in range(4):
+            if s < 3:
+                dq_send(3 - s).start()
+                dk_send(3 - s).start()
             products(s, 1)
-            if s:
-                dq_send(s).start()
-                dk_send(s).start()
     elif split > 1:
         vg_rest(3)
         products(3, 0)
@@ -725,13 +725,14 @@
 ):
     pairs = [(dq_in, dq_v, dq), (dk_in, dk_v, dk), (dv_in, dv_v, dv)]
     loads = [pltpu.make_async_copy(fac_in, fac_ref, in_sem.at[5]), pltpu.make_async_copy(sc_in, sc_v, in_sem.at[3]), pltpu.make_async_copy(w_in, w_v, in_sem.at[4])]
-    for copy in loads:
-        copy.start()
     ins = [pltpu.make_async_copy(a, b, in_sem.at[i]) for i, (a, b, _) in enumerate(pairs)]
     outs = [pltpu.make_async_copy(b, d, out_sem.at[i]) for i, (_, b, d) in enumerate(pairs)]
     outs += [pltpu.make_async_copy(new_v, new, out_sem.at[3]), pltpu.make_async_copy(upd_v, upd, out_sem.at[4])]
-    for copy in ins:
+    for copy in ins + loads:
         copy.start()
+    for i in range(3):
+        ins[i].wait()
+        outs[i].start()
     for copy in loads:
         copy.wait()
     update = sc_v[...] * fac_ref[0:1, 0:1]
@@ -739,9 +740,6 @@
     outs[4].start()
     new_v[...] = (w_v[...].astype(F32) - LEARN_RATE * update).astype(BF16)
     outs[3].start()
-    for i in range(3):
-        ins[i].wait()
-        outs[i].start()
     for copy in outs:
         copy.wait()
 

time: 94.2 us -> 93.9 us (level)
  no operation moved by 1% of the time
where the time goes in v5:
time: 93.9 us; the launch traced here: 93.7 us
  Pallas kernels  93.1 us (99%)
    pallas_call x1, Pallas kernels, fused(): pl.pallas_call(functools.partial(fused_kernel, pn), out_shape=[jax.ShapeD...  90.2 us
    pallas_call x1, Pallas kernels, finish(): pl.pallas_call(finish_kernel, out_shape=[jax.ShapeDtypeStruct(x.shape, x....  2.86 us

profile of v5, /device:TPU:0, one launch (start us, length us, event | category | flops | bytes accessed | tf_op | source)
XLA Modules:
  0.0 93.7 jit_solution(677818739308558078)
XLA Ops:
  0.6 90.2 %fused.1 = (bf16[384,1024]{1,0:T(8,128)(2,1)}, bf16[384,512]{1,0:T(8,128)(2,1)}, bf16[384,512]{1,0:T(8,128)(2,1)}, f32[336,512]{1,0:T(8,128)}, f32[8,128]{1,0:T(8,128)}) custom-call(s32[8]{0:T(128)} %lim_in.1, bf16[384,1024]{1,0:T(8,128)(2,1)} %q_ref.1, bf16[384,1024]{1,0:T(8,128)(2,1)} %g_ref.1, bf16[384,512]{1,0:T(8,128)(2,1)} %k_ref.1, ...), custom_call_target="tpu_custom_call" | custom-call | tf_op jit(solution)/shard_map/fused/pallas_call | solution.py:664
  90.9 2.9 %finish.1 = (bf16[384,1024]{1,0:T(8,128)(2,1)}, bf16[384,512]{1,0:T(8,128)(2,1)}, bf16[384,512]{1,0:T(8,128)(2,1)}, bf16[336,512]{1,0:T(8,128)(2,1)}, f32[336,512]{1,0:T(8,128)}) custom-call(bf16[384,1024]{1,0:T(8,128)(2,1)} %get-tuple-element.10.dq_in, bf16[384,512]{1,0:T(8,128)(2,1)} %get-tuple-element.11.dk_in, bf16[384,512]{1,0:T(8,128)(2,1)} %get-tuple-element.12.dv_in, ...), custom_call_target="tpu_custom_call" | custom-call | tf_op jit(solution)/shard_map/finish/pallas_call | solution.py:751

commit v6 on v5

--- a/solution.py
+++ b/solution.py
@@ -525,6 +525,9 @@
         for j in (1, 2, 3):
             vg_rest(j)
     products(0, 0)
+    weight_in.wait()
+    weight_f = wv[...].astype(F32)
+    weight_sum = jnp.sum(weight_f * weight_f)
     if split > 1:
         pass_on()
         if last:
@@ -579,9 +582,6 @@
         outs.append(local_out(vga.at[c], dv_ref, 2))
         outs[-1].start()
 
-    weight_in.wait()
-    weight_f = wv[...].astype(F32)
-    weight_sum = jnp.sum(weight_f * weight_f)
 
     early, late = list(range(min(3, pn.streams))), list(range(3, pn.streams))
     steps = [(s, 0, last) for s in early]

time: 93.9 us -> 93.7 us (level)
  no operation moved by 1% of the time
where the time goes in v6:
time: 93.7 us; the launch traced here: 93.6 us
  Pallas kernels  92.9 us (99%)
    pallas_call x1, Pallas kernels, fused(): pl.pallas_call(functools.partial(fused_kernel, pn), out_shape=[jax.ShapeD...  90.1 us
    pallas_call x1, Pallas kernels, finish(): pl.pallas_call(finish_kernel, out_shape=[jax.ShapeDtypeStruct(x.shape, x....  2.86 us

profile of v6, /device:TPU:0, one launch (start us, length us, event | category | flops | bytes accessed | tf_op | source)
XLA Modules:
  0.0 93.6 jit_solution(15443280626652268470)
XLA Ops:
  0.6 90.1 %fused.1 = (bf16[384,1024]{1,0:T(8,128)(2,1)}, bf16[384,512]{1,0:T(8,128)(2,1)}, bf16[384,512]{1,0:T(8,128)(2,1)}, f32[336,512]{1,0:T(8,128)}, f32[8,128]{1,0:T(8,128)}) custom-call(s32[8]{0:T(128)} %lim_in.1, bf16[384,1024]{1,0:T(8,128)(2,1)} %q_ref.1, bf16[384,1024]{1,0:T(8,128)(2,1)} %g_ref.1, bf16[384,512]{1,0:T(8,128)(2,1)} %k_ref.1, ...), custom_call_target="tpu_custom_call" | custom-call | tf_op jit(solution)/shard_map/fused/pallas_call | solution.py:664
  90.7 2.9 %finish.1 = (bf16[384,1024]{1,0:T(8,128)(2,1)}, bf16[384,512]{1,0:T(8,128)(2,1)}, bf16[384,512]{1,0:T(8,128)(2,1)}, bf16[336,512]{1,0:T(8,128)(2,1)}, f32[336,512]{1,0:T(8,128)}) custom-call(bf16[384,1024]{1,0:T(8,128)(2,1)} %get-tuple-element.10.dq_in, bf16[384,512]{1,0:T(8,128)(2,1)} %get-tuple-element.11.dk_in, bf16[384,512]{1,0:T(8,128)(2,1)} %get-tuple-element.12.dv_in, ...), custom_call_target="tpu_custom_call" | custom-call | tf_op jit(solution)/shard_map/finish/pallas_call | solution.py:751
